TPU v7x, 32 devices: a 4x4x1 block of a 4x4x8 slice. The times are simulated.
32 devices in a mesh: rep: 2 (over z, core), dp: 16 (over x, y).
Axes of the slice: x: 4, y: 4, z: 1, core: 2. Of those that a mesh axis runs over, the one named last changes fastest.
The devices are a block of a 4x4x8 slice.
Arguments:
- x: bfloat16 [32, 2048, 1024], P(('rep', 'dp')), parts along dimension 0
- dy: bfloat16 [32, 2048, 1024], P(('rep', 'dp')), parts along dimension 0
- w_gate: bfloat16 [2, 1024, 4096], replicated
- w_up: bfloat16 [2, 1024, 4096], replicated
- w_down: bfloat16 [2, 4096, 1024], replicated
- m_w_gate: float32 [2, 1024, 4096], P(None, 'dp')
- m_w_up: float32 [2, 1024, 4096], P(None, 'dp')
- m_w_down: float32 [2, 4096, 1024], P(None, 'dp')
- v_w_gate: float32 [2, 1024, 4096], P(None, 'dp')
- v_w_up: float32 [2, 1024, 4096], P(None, 'dp')
- v_w_down: float32 [2, 4096, 1024], P(None, 'dp')
Outputs:
- output 1: bfloat16 [4, 1024, 4096], P('rep'), parts along dimension 0
- output 2: bfloat16 [4, 1024, 4096], P('rep'), parts along dimension 0
- output 3: bfloat16 [4, 4096, 1024], P('rep'), parts along dimension 0
- output 4: float32 [4, 1024, 4096], P('rep', 'dp'), parts along dimension 0
- output 5: float32 [4, 1024, 4096], P('rep', 'dp'), parts along dimension 0
- output 6: float32 [4, 4096, 1024], P('rep', 'dp'), parts along dimension 0
- output 7: float32 [4, 1024, 4096], P('rep', 'dp'), parts along dimension 0
- output 8: float32 [4, 1024, 4096], P('rep', 'dp'), parts along dimension 0
- output 9: float32 [4, 4096, 1024], P('rep', 'dp'), parts along dimension 0
There are 2 independent parts. A program takes and returns all parts, laid end to end along the dimension named above; an argument that names none is the same for every part.
All inputs are finite; a program needn't handle non-finite values.
Results may differ from a plain program's by a relative error of at most 0.022.
Values are sent between devices in bfloat16 or wider.
A program may use at most 768 MiB of HBM per device.

v0:
```python
import jax
import jax.numpy as jnp
from jax import lax

NAMES = ("w_gate", "w_up", "w_down")


def matmul(a, w):
    return jnp.dot(a, w, preferred_element_type=jnp.float32).astype(jnp.bfloat16)


def normed(h):
    wide = h.astype(jnp.float32)
    scale = lax.rsqrt(jnp.mean(wide**2, -1, keepdims=True) + 1e-6)
    return (wide * scale).astype(jnp.bfloat16)


def layer(h, w):
    a = normed(h)
    gate = jnp.dot(a, w["w_gate"], preferred_element_type=jnp.float32)
    up = jnp.dot(a, w["w_up"], preferred_element_type=jnp.float32)
    return h + matmul((jax.nn.silu(gate) * up).astype(jnp.bfloat16), w["w_down"])


def adamw(w, m, v, g):
    m = 0.9 * m + 0.1 * g
    v = 0.95 * v + 0.05 * g * g
    step = m * lax.rsqrt(v + 1e-8) + 0.1 * w
    return (w - 0.02 * step).astype(jnp.bfloat16), m, v


def stack(weights, h):
    for number in range(weights["w_gate"].shape[0]):
        h = layer(h, {name: w[number] for name, w in weights.items()})
    return h


def solution(mesh):
    groups = mesh.shape["rep"]

    def step(x, dy, *arrays):
        weights, m, v = (arrays[i : i + 3] for i in (0, 3, 6))
        x, dy = (t.reshape(groups, -1, *t.shape[1:]) for t in (x, dy))

        def of_a_group(x, dy):
            _, back = jax.vjp(lambda w: stack(w, x), dict(zip(NAMES, weights, strict=True)))
            by_weights = back(dy)[0]
            gradients = [by_weights[name].astype(jnp.float32) for name in NAMES]
            new = [adamw(w.astype(jnp.float32), m, v, g) for w, m, v, g in zip(weights, m, v, gradients, strict=True)]
            return tuple(one[which] for which in range(3) for one in new)

        return tuple(t.reshape(-1, *t.shape[2:]) for t in jax.vmap(of_a_group)(x, dy))

    return step
```

profile of v0, /device:TPU:97, one launch (start us, length us, event | category | flops | bytes accessed | tf_op | source)
XLA Modules:
  0.0 1247.7 jit_solution(449904192534578816)
XLA Ops:
  10.3 6.5 copy
  16.9 24.5 %fusion.67 = f32[2048,4096]{1,0:T(8,128)} fusion(bf16[2,1024,4096]{2,1,0:T(8,128)(2,1)} %param, bf16[1,2048,1024]{2,1,0:T(8,128)(2,1)} %param.2, f32[2048]{0:T(1024)S(1)} %add_rsqrt_fusion), kind=kOutput, calls=%fused_computation.78 | convolution fusion | flops 17186160640 | bytes 46145536 | tf_op jit(solution)/vmap(jvp())/dot_general | solution.py:20
  41.4 23.4 %fusion.65 = f32[2048,4096]{1,0:T(8,128)} fusion(bf16[2,1024,4096]{2,1,0:T(8,128)(2,1)} %param.3, bf16[1,2048,1024]{2,1,0:T(8,128)(2,1)S(1)} %copy-done.2, f32[2048]{0:T(1024)S(1)} %add_rsqrt_fusion), kind=kOutput, calls=%fused_computation.76 | convolution fusion | flops 17186160640 | bytes 46145536 | tf_op jit(solution)/vmap(jvp())/dot_general | solution.py:21
  64.8 27.5 %fusion.26 = bf16[2048,4096]{1,0:T(8,128)(2,1)} fusion(f32[2048,4096]{1,0:T(8,128)} %fusion.65, f32[2048,4096]{1,0:T(8,128)} %fusion.67), kind=kLoop, calls=%fused_computation.35 | loop fusion | flops 50331648 | bytes 83886080
  92.3 24.0 %fusion.51 = (f32[2048]{0:T(1024)S(1)}, bf16[1,1,2048,1024]{2,3,1,0:T(8,128)(2,1)S(1)}) fusion(bf16[2048,4096]{1,0:T(8,128)(2,1)} %fusion.26, bf16[2,4096,1024]{2,1,0:T(8,128)(2,1)} %param.4, bf16[1,2048,1024]{1,2,0:T(8,128)(2,1)} %copy), kind=kOutput, calls=%fused_computation.62 | convolution fusion | flops 17190352896 | bytes 33562624 | tf_op jit(solution)/vmap(jvp())/dot_general | solution.py:9
  117.0 24.1 %fusion.54 = f32[2048,4096]{1,0:T(8,128)} fusion(bf16[2,1024,4096]{2,1,0:T(8,128)(2,1)} %param, bf16[1,1,2048,1024]{2,3,1,0:T(8,128)(2,1)S(1)} %get-tuple-element.10, f32[2048]{0:T(1024)S(1)} %bitcast.337), kind=kOutput, calls=%fused_computation.65 | convolution fusion | flops 17186160640 | bytes 46145536 | tf_op jit(solution)/vmap(jvp())/dot_general | solution.py:20
  141.1 23.6 %fusion.58 = f32[2048,4096]{1,0:T(8,128)} fusion(bf16[2,1024,4096]{2,1,0:T(8,128)(2,1)} %param.3, bf16[1,1,2048,1024]{2,3,1,0:T(8,128)(2,1)S(1)} %get-tuple-element.10, f32[2048]{0:T(1024)S(1)} %bitcast.338), kind=kOutput, calls=%fused_computation.69 | convolution fusion | flops 17186160640 | bytes 46145536 | tf_op jit(solution)/vmap(jvp())/dot_general | solution.py:21
  164.7 32.2 %fusion.35 = f32[1,4096,1024]{2,1,0:T(8,128)} fusion(f32[2048,4096]{1,0:T(8,128)} %fusion.58, f32[2048,4096]{1,0:T(8,128)} %fusion.54, bf16[1,2048,1024]{2,1,0:T(8,128)(2,1)} %param.5), kind=kOutput, calls=%fused_computation.52 | convolution fusion | flops 17230200832 | bytes 88080384 | tf_op jit(solution)/vmap(transpose(jvp()))/dot_general | solution.py:9
  197.0 6.8 copy.1
  203.8 24.4 %convolution_convert_fusion.1 = bf16[2048,4096]{1,0:T(8,128)(2,1)} fusion(bf16[2,4096,1024]{2,1,0:T(8,128)(2,1)} %param.4, bf16[1,2048,1024]{2,1,0:T(8,128)(2,1)} %param.5), kind=kOutput, calls=%fused_computation.44 | convolution fusion | flops 17188257792 | bytes 29360128 | tf_op jit(solution)/vmap(transpose(jvp()))/dot_general | solution.py:9
  228.2 32.9 %fusion.6 = bf16[2048,4096]{1,0:T(8,128)(2,1)} fusion(f32[2048,4096]{1,0:T(8,128)} %fusion.54, f32[2048,4096]{1,0:T(8,128)} %fusion.58, bf16[2048,4096]{1,0:T(8,128)(2,1)} %convolution_convert_fusion.1), kind=kLoop, calls=%fused_computation.11 | loop fusion | flops 100663296 | bytes 100663296
  261.1 27.0 %fusion.24 = bf16[2048,1024]{0,1:T(8,128)(2,1)} fusion(bf16[2048,4096]{1,0:T(8,128)(2,1)} %convolution_convert_fusion.1, f32[2048,4096]{1,0:T(8,128)} %fusion.54, bf16[2,1024,4096]{2,1,0:T(8,128)(2,1)} %param.3), kind=kOutput, calls=%fused_computation.34 | convolution fusion | flops 17230200832 | bytes 62914560 | tf_op jit(solution)/vmap(transpose(jvp()))/dot_general | solution.py:21
  288.1 25.0 %fusion.53 = (f32[2048]{0:T(1024)S(1)}, bf16[2048,1024]{0,1:T(8,128)(2,1)S(1)}) fusion(bf16[1,1,2048,1024]{2,3,1,0:T(8,128)(2,1)} %copy-done.3, bf16[2048,1024]{0,1:T(8,128)(2,1)} %fusion.24, bf16[2048,4096]{1,0:T(8,128)(2,1)} %fusion.6, bf16[2,1024,4096]{2,1,0:T(8,128)(2,1)} %param), kind=kOutput, calls=%fused_computation.64 | convolution fusion | flops 17190352896 | bytes 37756928 | tf_op jit(solution)/vmap(transpose(jvp()))/dot_general | solution.py:20
  318.4 22.4 %convolution_bitcast_fusion = f32[1,4096,1024]{2,1,0:T(8,128)} fusion(bf16[2048,4096]{1,0:T(8,128)(2,1)} %fusion.26, bf16[2048,1024]{0,1:T(8,128)(2,1)S(1)} %fusion.81), kind=kOutput, calls=%fused_computation.56 | convolution fusion | flops 17179869184 | bytes 37748736 | tf_op jit(solution)/vmap(transpose(jvp()))/dot_general | solution.py:9
  340.9 23.8 %convolution_bitcast_fusion.1 = f32[1,1024,4096]{2,1,0:T(8,128)} fusion(bf16[2048,4096]{1,0:T(8,128)(2,1)} %fusion.6, bf16[1,1,2048,1024]{2,3,1,0:T(8,128)(2,1)} %copy-done.3, f32[2048]{0:T(1024)S(1)} %bitcast.340), kind=kOutput, calls=%fused_computation.57 | convolution fusion | flops 17186160640 | bytes 37756928 | tf_op jit(solution)/vmap(transpose(jvp()))/dot_general | solution.py:20
  364.8 24.8 %convolution_convert_fusion = bf16[2048,4096]{1,0:T(8,128)(2,1)} fusion(bf16[2048,1024]{0,1:T(8,128)(2,1)} %copy-done.5, bf16[2,4096,1024]{2,1,0:T(8,128)(2,1)} %param.4), kind=kOutput, calls=%fused_computation.43 | convolution fusion | flops 17188257792 | bytes 29360128 | tf_op jit(solution)/vmap(transpose(jvp()))/dot_general | solution.py:9
  389.7 39.0 %fusion.41 = f32[1,1024,4096]{2,1,0:T(8,128)} fusion(f32[2048,4096]{1,0:T(8,128)} %fusion.67, f32[2048,4096]{1,0:T(8,128)} %fusion.65, bf16[2048,4096]{1,0:T(8,128)(2,1)} %convolution_convert_fusion, bf16[1,2048,1024]{1,2,0:T(8,128)(2,1)} %copy, f32[2048]{0:T(1024)S(1)} %copy-done.13), kind=kOutput, calls=%fused_computation.54 | convolution fusion | flops 17278435328 | bytes 104865792 | tf_op jit(solution)/vmap(transpose(jvp()))/dot_general | solution.py:20
  428.8 29.4 %fusion.38 = f32[1,1024,4096]{2,1,0:T(8,128)} fusion(bf16[2048,4096]{1,0:T(8,128)(2,1)} %convolution_convert_fusion.1, f32[2048,4096]{1,0:T(8,128)} %fusion.54, bf16[1,1,2048,1024]{2,3,1,0:T(8,128)(2,1)} %copy-done.3, f32[2048]{0:T(1024)S(1)} %bitcast.341), kind=kOutput, calls=%fused_computation.53 | convolution fusion | flops 17236492288 | bytes 71311360 | tf_op jit(solution)/vmap(transpose(jvp()))/dot_general | solution.py:21
  458.3 29.6 %fusion.44 = f32[1,1024,4096]{2,1,0:T(8,128)} fusion(bf16[2048,4096]{1,0:T(8,128)(2,1)} %convolution_convert_fusion, f32[2048,4096]{1,0:T(8,128)} %fusion.67, bf16[1,2048,1024]{1,2,0:T(8,128)(2,1)} %copy, f32[2048]{0:T(1024)S(1)} %copy-done.13), kind=kOutput, calls=%fused_computation.55 | convolution fusion | flops 17236492288 | bytes 71311360 | tf_op jit(solution)/vmap(transpose(jvp()))/dot_general | solution.py:21
  492.5 5.4 fusion.121
  498.1 59.8 %reduce-scatter.19.cloned.1.call-done = f32[1,64,4096]{2,1,0:T(8,128)} async-done(((f32[1,1024,4096]{2,1,0:T(8,128)}), f32[1,64,4096]{2,1,0:T(8,128)}) %reduce-scatter.19.cloned.1.call-update) | async-done | bytes 1048592
  559.1 107.3 %reduce-scatter.21.cloned.1.call-done = f32[1,64,4096]{2,1,0:T(8,128)} async-done(((f32[1,1024,4096]{2,1,0:T(8,128)}), f32[1,64,4096]{2,1,0:T(8,128)}) %reduce-scatter.21.cloned.1.call-update) | async-done | bytes 1048592
  667.7 6.0 fusion.123
  673.8 100.6 %reduce-scatter.23.cloned.1.call-done = f32[1,64,4096]{2,1,0:T(8,128)} async-done(((f32[1,1024,4096]{2,1,0:T(8,128)}), f32[1,64,4096]{2,1,0:T(8,128)}) %reduce-scatter.23.cloned.1.call-update) | async-done | bytes 1048592
  775.7 107.3 %reduce-scatter.25.cloned.1.call-done = f32[1,64,4096]{2,1,0:T(8,128)} async-done(((f32[1,1024,4096]{2,1,0:T(8,128)}), f32[1,64,4096]{2,1,0:T(8,128)}) %reduce-scatter.25.cloned.1.call-update) | async-done | bytes 1048592
  884.3 5.3 fusion.122
  889.7 101.0 %all-gather.14.cloned.1.call-done = bf16[1,2,4096,1024]{3,2,1,0:T(8,128)(2,1)} async-done(((bf16[1,2,256,1024]{3,2,1,0:T(8,128)(2,1)}), bf16[1,2,4096,1024]{3,2,1,0:T(8,128)(2,1)}) %all-gather.14.cloned.1.call-update) | async-done | bytes 16777232 | tf_op jit(solution)/reshape | solution.py:52
  990.7 107.9 %all-gather.10.cloned.1.call-done = bf16[1,2,1024,4096]{3,2,1,0:T(8,128)(2,1)} async-done(((bf16[1,2,64,4096]{3,2,1,0:T(8,128)(2,1)}), bf16[1,2,1024,4096]{3,2,1,0:T(8,128)(2,1)}) %all-gather.10.cloned.1.call-update) | async-done | bytes 16777232 | tf_op jit(solution)/reshape | solution.py:52
  1098.6 108.0 %all-gather.12.cloned.1.call-done = bf16[1,2,1024,4096]{3,2,1,0:T(8,128)(2,1)} async-done(((bf16[1,2,64,4096]{3,2,1,0:T(8,128)(2,1)}), bf16[1,2,1024,4096]{3,2,1,0:T(8,128)(2,1)}) %all-gather.12.cloned.1.call-update) | async-done | bytes 16777232 | tf_op jit(solution)/reshape | solution.py:52
  1206.6 16.8 %copy.5 = bf16[2,1024,4096]{2,1,0:T(8,128)(2,1)} copy(bf16[2,1024,4096]{2,1,0:T(8,128)(2,1)} %bitcast.332) | data formatting | bytes 33554432
  1223.4 8.5 copy.6
  1234.5 6.2 copy.7
  (72 shorter events, 21.5 us)
Async XLA Ops:
  7.2 482.7 %reduce-scatter.27.cloned.1.call-start = ((), (), s32[]{:S(2)}) async-start(), calls=%async_computation.13 | async-start | bytes 17825792
  16.9 24.6 %copy-start.12 = (f32[2048]{0:T(1024)}, f32[2048]{0:T(1024)S(1)}, u32[]{:S(2)}) copy-start(f32[2048]{0:T(1024)S(1)} %add_rsqrt_fusion) | copy-start | bytes 24580
  16.9 24.6 %copy-start.2 = (bf16[1,2048,1024]{2,1,0:T(8,128)(2,1)S(1)}, bf16[1,2048,1024]{2,1,0:T(8,128)(2,1)}, u32[]{:S(2)}) copy-start(bf16[1,2048,1024]{2,1,0:T(8,128)(2,1)} %param.2) | copy-start | bytes 12582916
  116.3 24.8 %copy-start.3 = (bf16[1,1,2048,1024]{2,3,1,0:T(8,128)(2,1)}, bf16[1,1,2048,1024]{2,3,1,0:T(8,128)(2,1)S(1)}, u32[]{:S(2)}) copy-start(bf16[1,1,2048,1024]{2,3,1,0:T(8,128)(2,1)S(1)} %get-tuple-element.10) | copy-start | bytes 12582916
  116.3 0.7 copy-start.8
  117.0 24.1 %copy-start.10 = (f32[1,1,2048]{2,1,0:T(1,128)}, f32[1,1,2048]{2,1,0:T(1,128)S(1)}, u32[]{:S(2)}) copy-start(f32[1,1,2048]{2,1,0:T(1,128)S(1)} %rsqrt.31) | copy-start | bytes 24580
  197.0 294.2 %reduce-scatter.29.cloned.1.call-start = ((), (), s32[]{:S(2)}) async-start(), calls=%async_computation.14 | async-start | bytes 17825792
  288.1 25.0 %copy-start.9 = (f32[2048]{0:T(1024)S(1)}, f32[2048]{0:T(1024)}, u32[]{:S(2)}) copy-start(f32[2048]{0:T(1024)} %copy-done.8) | copy-start | bytes 24580
  288.1 25.1 %copy-start = (bf16[1,2048,1024]{1,2,0:T(8,128)(2,1)S(1)}, bf16[1,2048,1024]{1,2,0:T(8,128)(2,1)}, u32[]{:S(2)}) copy-start(bf16[1,2048,1024]{1,2,0:T(8,128)(2,1)} %copy.1) | copy-start | bytes 12582916
  288.1 25.1 %copy-start.4 = (bf16[1,1,2048,1024]{2,3,1,0:T(8,128)(2,1)S(1)}, bf16[1,1,2048,1024]{2,3,1,0:T(8,128)(2,1)}, u32[]{:S(2)}) copy-start(bf16[1,1,2048,1024]{2,3,1,0:T(8,128)(2,1)} %copy-done.3) | copy-start | bytes 12582916
  288.1 25.1 %copy-start.11 = (f32[1,1,2048]{2,1,0:T(1,128)S(1)}, f32[1,1,2048]{2,1,0:T(1,128)}, u32[]{:S(2)}) copy-start(f32[1,1,2048]{2,1,0:T(1,128)} %copy-done.10) | copy-start | bytes 24580
  316.4 2.0 copy-start.5
  340.9 217.0 %reduce-scatter.19.cloned.1.call-start = ((), (), s32[]{:S(2)}) async-start(), calls=%async_computation.9 | async-start | bytes 17825792
  364.8 24.9 %copy-start.13 = (f32[2048]{0:T(1024)S(1)}, f32[2048]{0:T(1024)}, u32[]{:S(2)}) copy-start(f32[2048]{0:T(1024)} %copy-done.12) | copy-start | bytes 24580
  364.8 301.6 %reduce-scatter.21.cloned.1.call-start = ((), (), s32[]{:S(2)}) async-start(), calls=%async_computation.10 | async-start | bytes 17825792
  428.8 345.7 %reduce-scatter.23.cloned.1.call-start = ((), (), s32[]{:S(2)}) async-start(), calls=%async_computation.11 | async-start | bytes 17825792
  458.3 424.7 %reduce-scatter.25.cloned.1.call-start = ((), (), s32[]{:S(2)}) async-start(), calls=%async_computation.12 | async-start | bytes 17825792
  488.0 0.7 copy-start.14
  488.0 4.6 copy-start.6
  488.0 502.7 %all-gather.14.cloned.1.call-start = ((), (), s32[]{:S(2)}) async-start(), calls=%async_computation.8 | async-start | bytes 17825792 | tf_op jit(solution)/reshape | solution.py:52
  498.0 600.7 %all-gather.10.cloned.1.call-start = ((), (), s32[]{:S(2)}) async-start(), calls=%async_computation.6 | async-start | bytes 17825792 | tf_op jit(solution)/reshape | solution.py:52
  559.1 325.2 %copy-start.7 = (f32[2,64,4096]{2,1,0:T(8,128)S(1)}, f32[2,64,4096]{2,1,0:T(8,128)}, u32[]{:S(2)}) copy-start(f32[2,64,4096]{2,1,0:T(8,128)} %param.8) | copy-start | bytes 6291460
  673.7 532.8 %all-gather.12.cloned.1.call-start = ((), (), s32[]{:S(2)}) async-start(), calls=%async_computation.7 | async-start | bytes 17825792 | tf_op jit(solution)/reshape | solution.py:52
  1206.6 16.8 %copy-start.1 = (bf16[1,2,1024,4096]{3,2,1,0:T(8,128)(2,1)S(1)}, bf16[1,2,1024,4096]{3,2,1,0:T(8,128)(2,1)}, u32[]{:S(2)}) copy-start(bf16[1,2,1024,4096]{3,2,1,0:T(8,128)(2,1)} %all-gather.12.cloned.1.call-done) | copy-start | bytes 50331652
  1206.6 25.3 %slice-start = ((s8[16777216]{0:T(1024)(128)(4,1)}), s8[4194304]{0:T(1024)(128)(4,1)S(1)}, s32[]{:S(2)}) async-start(s8[16777216]{0:T(1024)(128)(4,1)} %bitcast.329), calls=%async_computation.15 | async-start | bytes 8388608
  1206.6 25.3 %slice-start.1 = ((s8[16777216]{0:T(1024)(128)(4,1)}), s8[4194304]{0:T(1024)(128)(4,1)S(1)}, s32[]{:S(2)}) async-start(s8[16777216]{0:T(1024)(128)(4,1)} %bitcast.329), calls=%async_computation.16 | async-start | bytes 8388608
  1223.4 9.9 slice-start.2
  1223.4 11.1 slice-start.3
Sparse Core Ops, SparseCore 0:
  197.1 108.6 reduce-scatter.26
  341.0 108.6 reduce-scatter.28
  452.9 104.9 reduce-scatter.18
  561.5 104.8 reduce-scatter.20
  669.5 104.8 reduce-scatter.22
  778.1 104.8 reduce-scatter.24
  885.0 105.6 all-gather.13
  993.3 105.3 all-gather.9
  1101.2 105.3 all-gather.11
where the time goes:
time: 1260 us; the launch traced here: 1250 us
  waiting for transfers between devices  692 us (55%)
  matrix products  397 us (32%)
  other arithmetic  91.1 us (7%)
  local copies, waits for them, and re-layouts  51.2 us (4%)
  between operations  15.2 us (1%)
    unnamed x15, waiting for transfers between devices  376 us
    reshape x3, waiting for transfers between devices, step(): t.reshape(-1, *t.shape[2:])  317 us
    dot_general x5, matrix products, layer(): gate = jnp.dot(a, w['w_gate'], preferred_element_type=jnp.float32)  136 us
    dot_general x5, matrix products, layer(): up = jnp.dot(a, w['w_up'], preferred_element_type=jnp.float32)  133 us
    dot_general x5, matrix products, matmul(): jnp.dot(a, w, preferred_element_type=jnp.float32).astype(jnp.bfloat16)  128 us
    unnamed x4, other arithmetic  63.6 us
    unnamed x43, local copies, waits for them, and re-layouts  50.6 us
  transfers between devices with their start and end apart: 9, of which 7 were waited for; matrix products, arithmetic and copies ran while one was open for 25% of the time, Pallas kernels for 0%

commit v1 on v0

v1 whole, which is shorter than its diff:
```python
import functools
import math

import jax
import jax.numpy as jnp
from jax import lax
from jax.experimental import pallas as pl
from jax.experimental.pallas import tpu as pltpu
from jax.sharding import PartitionSpec as P

F32, BF16 = jnp.float32, jnp.bfloat16
MESH = pl.DeviceIdType.MESH
VMEM_LIMIT = 64 * 1024 * 1024 - 128 * 1024
FLOWS = 4
HOPS = 3
ROW_TILES = 4


def mm(a, b, dims=((1,), (0,))):
    return lax.dot_general(a, b, (dims, ((), ())), preferred_element_type=F32)


def scale_of(wide):
    return lax.rsqrt(jnp.mean(wide**2, -1, keepdims=True) + 1e-6)


def adamw(w, m, v, g):
    m = 0.9 * m + 0.1 * g
    v = 0.95 * v + 0.05 * g * g
    step = m * lax.rsqrt(v + 1e-8) + 0.1 * w
    return (w - 0.02 * step).astype(BF16), m, v


class Sizes:
    def __init__(self, tokens, d, ff, layers, group):
        self.tokens, self.d, self.ff, self.layers, self.group = tokens, d, ff, layers, group
        self.side = math.isqrt(group)
        self.rows = d // group
        self.quarters = ff // group // self.rows
        assert self.quarters == FLOWS and self.side == HOPS + 1
        self.cols = d // 4
        self.fb = 2 * self.cols
        self.gu_units = ff // self.fb
        self.d_units = d // self.cols
        self.per_layer = self.gu_units + self.d_units
        self.units = layers * self.per_layer


def step_kernel(
    z,
    h1_in, a1_in, a0_in, dy_in, wg_in, wu_in, wd_in, mg_in, mu_in, md_in, vg_in, vu_in, vd_in,
    w_out, g_out, dgu_hbm, pt_hbm,
    a, at, d, da, wg, wu, wd, dgu, pt, grads,
    hrecv, hsend, hsum, lrecv, lsend, w_new, g_own, w_old, m_old, v_old,
    hs, hr, ls, lr, als, alr, ahs, ahr, own_sem, g_sem, adam_sem, w_sem, in_sem, dgu_sem, pt_sem,
):
    side, rows, cols, fb = z.side, z.rows, z.cols, z.fb
    rep, me = lax.axis_index("rep"), lax.axis_index("dp")
    cx, cy = me // side, me % side
    first = [cx, cx, cy, cy]
    second = [cy, cy, cx, cx]
    way = [1, -1, 1, -1]

    def device(x, y):
        return (rep, ((x + side) % side) * side + (y + side) % side)

    def next_on_first(f):
        return device(cx + way[f], cy) if f < 2 else device(cx, cy + way[f])

    def next_on_second(f):
        return device(cx, cy + way[f]) if f < 2 else device(cx + way[f], cy)

    def behind(at_, f, n):
        return (at_ - way[f] * n + 2 * side) % side

    def remote(src, dst, send, recv, target):
        return pltpu.make_async_remote_copy(src, dst, send, recv, device_id=target, device_id_type=MESH)

    def h_copy(u, s, f):
        par = u % 2
        src = grads.at[u % 3, f, pl.ds(side * behind(first[f], f, 1), side)] if s == 0 else hsend.at[par, s - 1, f]
        return remote(src, hrecv.at[par, s, f], hs.at[par, s, f], hr.at[par, s, f], next_on_first(f))

    def l_copy(u, s, f):
        par = u % 2
        return remote(lsend.at[par, s, f], lrecv.at[par, s, f], ls.at[par, s, f], lr.at[par, s, f], next_on_second(f))

    def al_copy(u, s, f):
        par = u % 2
        place = side * first[f] + behind(second[f], f, s)
        dst = w_out.at[u, f, place]
        src = w_new.at[par, f] if s == 0 else dst
        return remote(src, dst, als.at[par, s, f], alr.at[par, s, f], next_on_second(f))

    def ah_copy(u, s, f):
        par = u % 2
        dst = w_out.at[u, f, pl.ds(side * behind(first[f], f, s), side)]
        return remote(dst, dst, ahs.at[par, s, f], ahr.at[par, s, f], next_on_first(f))

    def own_copy(u, f):
        return pltpu.make_async_copy(w_new.at[u % 2, f], w_out.at[u, f, side * first[f] + second[f]], own_sem.at[u % 2, f])

    def g_copy(u):
        return pltpu.make_async_copy(g_own.at[u % 2], g_out.at[u], g_sem.at[u % 2])

    def place_of(u):
        return z.layers - 1 - u // z.per_layer, u % z.per_layer

    def adam_loads(u, start):
        layer, k = place_of(u) if start else (0, 0)

        def go(copies):
            for c in copies:
                c.start()

        def copies_gu():
            c0 = pl.multiple_of(k * fb, fb)
            r0 = pl.multiple_of(me * rows, rows)
            out = []
            for f in range(FLOWS):
                col = pl.ds(c0 + (f % 2) * cols, cols)
                w_, m_, v_ = ((wg_in, mg_in, vg_in), (wu_in, mu_in, vu_in))[f // 2]
                out.append(pltpu.make_async_copy(w_.at[layer, pl.ds(r0, rows), col], w_old.at[f], adam_sem.at[0, f]))
                out.append(pltpu.make_async_copy(m_.at[layer, :, col], m_old.at[f], adam_sem.at[1, f]))
                out.append(pltpu.make_async_copy(v_.at[layer, :, col], v_old.at[f], adam_sem.at[2, f]))
            return out

        def copies_d():
            col = pl.ds(pl.multiple_of((k - z.gu_units) * cols, cols), cols)
            out = []
            for f in range(FLOWS):
                r0 = pl.multiple_of((me * FLOWS + f) * rows, rows)
                out.append(pltpu.make_async_copy(wd_in.at[layer, pl.ds(r0, rows), col], w_old.at[f], adam_sem.at[0, f]))
                out.append(pltpu.make_async_copy(md_in.at[layer, pl.ds(f * rows, rows), col], m_old.at[f], adam_sem.at[1, f]))
                out.append(pltpu.make_async_copy(vd_in.at[layer, pl.ds(f * rows, rows), col], v_old.at[f], adam_sem.at[2, f]))
            return out

        if start:
            pl.when(k < z.gu_units)(lambda: go(copies_gu()))
            pl.when(k >= z.gu_units)(lambda: go(copies_d()))
        else:
            for c in copies_gu():
                c.wait()

    def both(x, y):
        return x.astype(F32) + y.astype(F32)

    def h_hop(u, s):
        par, slot = u % 2, u % 3
        if s:
            for f in range(FLOWS):
                h_copy(u, s - 1, f).wait_recv()
                mine = grads[slot, f, pl.ds(side * behind(first[f], f, s + 1), side)]
                hsend[par, s - 1, f] = both(hrecv[par, s - 1, f], mine).astype(BF16)
        for f in range(FLOWS):
            h_copy(u, s, f).start()
            if s == HOPS - 1:
                h_copy(u, 0, f).wait_send()

    def h_end_l_start(u):
        par, slot = u % 2, u % 3
        for f in range(FLOWS):
            h_copy(u, HOPS - 1, f).wait_recv()
            hsum[par, f] = both(hrecv[par, HOPS - 1, f], grads[slot, f, pl.ds(side * first[f], side)])
            lsend[par, 0, f] = hsum[par, f, behind(second[f], f, 1)].astype(BF16)
        for f in range(FLOWS):
            l_copy(u, 0, f).start()
        for f in range(FLOWS):
            for s in range(1, HOPS):
                h_copy(u, s, f).wait_send()

    def l_hop(u, s):
        par = u % 2
        for f in range(FLOWS):
            l_copy(u, s - 1, f).wait_recv()
            lsend[par, s, f] = both(lrecv[par, s - 1, f], hsum[par, f, behind(second[f], f, s + 1)]).astype(BF16)
        for f in range(FLOWS):
            l_copy(u, s, f).start()

    def l_end_al_start(u):
        par = u % 2
        adam_loads(u, False)
        for f in range(FLOWS):
            l_copy(u, HOPS - 1, f).wait_recv()
            g = both(lrecv[par, HOPS - 1, f], hsum[par, f, second[f]]).astype(BF16)
            g_own[par, f] = g
            w_new[par, f] = adamw(w_old[f].astype(F32), m_old[f], v_old[f], g.astype(F32))[0]
        for f in range(FLOWS):
            al_copy(u, 0, f).start()
            own_copy(u, f).start()
        g_copy(u).start()
        for f in range(FLOWS):
            for s in range(HOPS):
                l_copy(u, s, f).wait_send()

    def al_hop(u, s):
        for f in range(FLOWS):
            al_copy(u, s - 1, f).wait_recv()
            al_copy(u, s, f).start()

    def al_end_ah_start(u):
        for f in range(FLOWS):
            al_copy(u, HOPS - 1, f).wait_recv()
            own_copy(u, f).wait()
            ah_copy(u, 0, f).start()
        for f in range(FLOWS):
            for s in range(HOPS):
                al_copy(u, s, f).wait_send()
        g_copy(u).wait()

    def ah_hop(u, s):
        for f in range(FLOWS):
            ah_copy(u, s - 1, f).wait_recv()
            ah_copy(u, s, f).start()

    def ah_end(u):
        for f in range(FLOWS):
            ah_copy(u, HOPS - 1, f).wait_recv()
            for s in range(HOPS):
                ah_copy(u, s, f).wait_send()

    def if_unit(u, step):
        pl.when((u >= 0) & (u < z.units))(lambda: step(u))

    def slot_0(h):
        if_unit(h, lambda u: h_hop(u, 0))
        if_unit(h - 8, ah_end)
        if_unit(h - 6, al_end_ah_start)
        if_unit(h - 4, l_end_al_start)
        if_unit(h - 2, h_end_l_start)

    def slot_1(h):
        if_unit(h - 1, lambda u: h_hop(u, 2))
        if_unit(h - 3, lambda u: l_hop(u, 2))
        if_unit(h - 5, lambda u: al_hop(u, 2))
        if_unit(h - 7, lambda u: ah_hop(u, 2))
        if_unit(h - 3, lambda u: adam_loads(u, True))

    def slot_2(h):
        if_unit(h, lambda u: h_hop(u, 1))
        if_unit(h - 2, lambda u: l_hop(u, 1))
        if_unit(h - 4, lambda u: al_hop(u, 1))
        if_unit(h - 6, lambda u: ah_hop(u, 1))

    tile = z.tokens // ROW_TILES

    def rows_of(t, size):
        return pl.ds(pl.multiple_of(t * size, size), size)

    def weight_loads(layer, j, buf, with_down):
        cols_j = pl.ds(pl.multiple_of(j * fb, fb), fb)
        out = [
            pltpu.make_async_copy(wg_in.at[layer, :, cols_j], wg.at[buf], w_sem.at[buf, 0]),
            pltpu.make_async_copy(wu_in.at[layer, :, cols_j], wu.at[buf], w_sem.at[buf, 1]),
        ]
        if with_down:
            out.append(pltpu.make_async_copy(wd_in.at[layer, cols_j, :], wd.at[buf], w_sem.at[buf, 2]))
        return out

    def backward_tile(t, buf):
        r = rows_of(t, tile)
        a_t = a[r, :]
        gate = mm(a_t, wg[buf])
        up = mm(a_t, wu[buf])
        dp = mm(d[r, :], wd[buf], ((1,), (1,))).astype(BF16).astype(F32)
        sig = jax.nn.sigmoid(gate)
        silu = gate * sig
        pt[0, :, r] = (silu * up).astype(BF16).T
        dgu[0, r, pl.ds(fb, fb)] = (dp * silu).astype(BF16)
        dgu[0, r, pl.ds(0, fb)] = (dp * up * (sig * (1 + gate * (1 - sig)))).astype(BF16)

    def keep_copies(j):
        return [
            pltpu.make_async_copy(pt.at[0], pt_hbm.at[j], pt_sem.at[0]),
            pltpu.make_async_copy(dgu.at[0], dgu_hbm.at[j], dgu_sem.at[0]),
        ]

    def store_block(slot, f, dev, value):
        x, y = dev // side, dev % side
        grads[slot, f, x * side + y if f < 2 else y * side + x] = value

    def gu_grads(m, slot):
        half = z.d // 2
        out = mm(at[rows_of(m, half), :], dgu[0]).astype(BF16)
        for n in range(z.group // 2):
            for f in range(FLOWS):
                store_block(slot, f, m * (z.group // 2) + n, out[n * rows : (n + 1) * rows, f * cols : (f + 1) * cols])

    def d_grads(t, i, slot):
        buf = t % 2
        pltpu.make_async_copy(pt_hbm.at[t], pt.at[buf], pt_sem.at[buf]).wait()
        out = mm(pt[buf], d[:, rows_of(i, cols)]).astype(BF16)
        devices = z.group // z.gu_units
        for n in range(devices):
            for f in range(FLOWS):
                r0 = (n * FLOWS + f) * rows
                store_block(slot, f, t * devices + n, out[r0 : r0 + rows])

        @pl.when(t + 2 < z.gu_units)
        def _():
            pltpu.make_async_copy(pt_hbm.at[t + 2], pt.at[buf], pt_sem.at[buf]).start()

    def d_first_loads():
        for t in range(2):
            pltpu.make_async_copy(pt_hbm.at[t], pt.at[t], pt_sem.at[t]).start()

    def da_tile(t, buf, fresh):
        r = rows_of(t, tile)
        part = mm(dgu[buf, r, pl.ds(0, fb)], wg[buf], ((1,), (1,))) + mm(dgu[buf, r, pl.ds(fb, fb)], wu[buf], ((1,), (1,)))

        @pl.when(fresh)
        def _():
            da[r, :] = part

        @pl.when(jnp.logical_not(fresh))
        def _():
            da[r, :] = da[r, :] + part

    def loop(lo, hi, body):
        lax.fori_loop(lo, hi, lambda i, c: (body(i), c)[1], 0)

    norm_tile = z.tokens // 16

    def norm_backward(t):
        r = rows_of(t, norm_tile)
        wide = a[r, :].astype(F32)
        scale = scale_of(wide)
        by_a = da[r, :].astype(BF16).astype(F32)
        inner = jnp.mean(by_a * wide, -1, keepdims=True)
        d[r, :] = both(d[r, :], (scale * by_a - wide * (scale**3 * inner)).astype(BF16)).astype(BF16)

    def transpose_tile(t):
        r = rows_of(t, norm_tile)
        at[:, r] = a[r, :].T

    last = z.layers - 1
    n_gu, n_d = z.gu_units, z.d_units
    a_end = n_gu - 1
    c_end = a_end + n_d
    a2_end = c_end + n_gu
    c2_end = a2_end + n_d
    per_c = n_gu // n_d

    def gu_index(h):
        return jnp.where(h < a_end, last, 0), jnp.where(h < a_end, h + 1, h - c_end)

    def piece_1(h):
        is_gu = (h < a_end) | ((h >= c_end) & (h < a2_end))
        is_d = ((h >= a_end) & (h < c_end)) | ((h >= a2_end) & (h < c2_end))
        layer, j = gu_index(h)

        @pl.when(h == c_end)
        def _():
            cp = pltpu.make_async_copy(a0_in, a, in_sem.at[0])
            cp.wait()
            loop(0, 16, transpose_tile)

        @pl.when(is_gu)
        def _():
            for c in weight_loads(layer, j, j % 2, True):
                c.wait()

            @pl.when(j + 1 < n_gu)
            def _():
                for c in weight_loads(layer, j + 1, (j + 1) % 2, True):
                    c.start()

            loop(0, ROW_TILES // 2, lambda t: backward_tile(t, j % 2))

        @pl.when((h >= a_end) & (h < c_end))
        def _():
            for b in range(per_c):
                blk = (h - a_end) * per_c + b
                for c in weight_loads(last, blk, b, False):
                    c.start()
                pltpu.make_async_copy(dgu_hbm.at[blk], dgu.at[b], dgu_sem.at[b]).start()

        @pl.when(h == a_end)
        def _():
            pltpu.make_async_copy(h1_in, a, in_sem.at[0]).start()

        @pl.when(is_d)
        def _():
            i = jnp.where(h < c_end, h - a_end, h - a2_end)
            d_first_loads()
            loop(0, n_gu // 2, lambda t: d_grads(t, i, (h + 1) % 3))

    def da_block(h, b):
        blk = (h - a_end) * per_c + b
        for c in weight_loads(last, blk, b, False):
            c.wait()
        pltpu.make_async_copy(dgu_hbm.at[blk], dgu.at[b], dgu_sem.at[b]).wait()
        loop(0, ROW_TILES, lambda t: da_tile(t, b, blk == 0))

    def piece_2(h):
        is_gu = (h < a_end) | ((h >= c_end) & (h < a2_end))
        is_d = ((h >= a_end) & (h < c_end)) | ((h >= a2_end) & (h < c2_end))
        layer, j = gu_index(h)

        @pl.when(is_gu)
        def _():
            loop(ROW_TILES // 2, ROW_TILES, lambda t: backward_tile(t, j % 2))

        @pl.when(is_d)
        def _():
            i = jnp.where(h < c_end, h - a_end, h - a2_end)
            loop(n_gu // 2, n_gu, lambda t: d_grads(t, i, (h + 1) % 3))

        @pl.when((h >= a_end) & (h < c_end))
        def _():
            da_block(h, 0)

    def piece_3(h):
        is_gu = (h < a_end) | ((h >= c_end) & (h < a2_end))
        layer, j = gu_index(h)

        @pl.when(is_gu)
        def _():
            for c in keep_copies(j):
                c.start()
            loop(0, 2, lambda m: gu_grads(m, (h + 1) % 3))
            for c in keep_copies(j):
                c.wait()

        @pl.when((h >= a_end) & (h < c_end))
        def _():
            for b in range(1, per_c):
                da_block(h, b)

        @pl.when(h == c_end - 1)
        def _():
            pltpu.make_async_copy(h1_in, a, in_sem.at[0]).wait()
            loop(0, 16, norm_backward)
            pltpu.make_async_copy(a0_in, a, in_sem.at[0]).start()
            for c in weight_loads(0, 0, 0, True):
                c.start()

    first_loads = [pltpu.make_async_copy(a1_in, a, in_sem.at[0]), pltpu.make_async_copy(dy_in, d, in_sem.at[1])]
    for c in first_loads + weight_loads(last, 0, 0, True) + weight_loads(last, 1, 1, True):
        c.start()
    barrier = pltpu.get_barrier_semaphore()
    for f in range(FLOWS):
        pl.semaphore_signal(barrier, inc=1, device_id=next_on_first(f), device_id_type=MESH)
    for c in first_loads + weight_loads(last, 0, 0, True):
        c.wait()
    loop(0, 16, transpose_tile)
    loop(0, ROW_TILES, lambda t: backward_tile(t, 0))
    for c in keep_copies(0):
        c.start()
    loop(0, 2, lambda m: gu_grads(m, 0))
    for c in keep_copies(0):
        c.wait()
    pl.semaphore_wait(barrier, FLOWS)

    def half_step(h):
        slot_0(h)
        piece_1(h)
        slot_1(h)
        piece_2(h)
        slot_2(h)
        piece_3(h)

    loop(0, z.units + 8, half_step)


def train_kernel_call(z, h1, a1, a0, dy, weights, moments):
    side, rows, cols, fb = z.side, z.rows, z.cols, z.fb
    dma = pltpu.SemaphoreType.DMA
    hbm = pl.BlockSpec(memory_space=pl.ANY)
    out_shape = (
        jax.ShapeDtypeStruct((z.units, FLOWS, z.group, rows, cols), BF16),
        jax.ShapeDtypeStruct((z.units, FLOWS, rows, cols), BF16),
        jax.ShapeDtypeStruct((z.gu_units, z.tokens, 2 * fb), BF16),
        jax.ShapeDtypeStruct((z.gu_units, fb, z.tokens), BF16),
    )
    scratch = [
        pltpu.VMEM((z.tokens, z.d), BF16),
        pltpu.VMEM((z.d, z.tokens), BF16),
        pltpu.VMEM((z.tokens, z.d), BF16),
        pltpu.VMEM((z.tokens, z.d), F32),
        pltpu.VMEM((2, z.d, fb), BF16),
        pltpu.VMEM((2, z.d, fb), BF16),
        pltpu.VMEM((2, fb, z.d), BF16),
        pltpu.VMEM((2, z.tokens, 2 * fb), BF16),
        pltpu.VMEM((2, fb, z.tokens), BF16),
        pltpu.VMEM((3, FLOWS, z.group, rows, cols), BF16),
        pltpu.VMEM((2, HOPS, FLOWS, side, rows, cols), BF16),
        pltpu.VMEM((2, HOPS - 1, FLOWS, side, rows, cols), BF16),
        pltpu.VMEM((2, FLOWS, side, rows, cols), F32),
        pltpu.VMEM((2, HOPS, FLOWS, rows, cols), BF16),
        pltpu.VMEM((2, HOPS, FLOWS, rows, cols), BF16),
        pltpu.VMEM((2, FLOWS, rows, cols), BF16),
        pltpu.VMEM((2, FLOWS, rows, cols), BF16),
        pltpu.VMEM((FLOWS, rows, cols), BF16),
        pltpu.VMEM((FLOWS, rows, cols), F32),
        pltpu.VMEM((FLOWS, rows, cols), F32),
        *[dma((2, HOPS, FLOWS)) for _ in range(8)],
        dma((2, FLOWS)),
        dma((2,)),
        dma((3, FLOWS)),
        dma((2, 3)),
        dma((2,)),
        dma((2,)),
        dma((2,)),
    ]
    return pl.pallas_call(
        functools.partial(step_kernel, z),
        out_shape=out_shape,
        in_specs=[hbm] * 13,
        out_specs=(hbm,) * 4,
        scratch_shapes=scratch,
        name="train_step",
        compiler_params=pltpu.CompilerParams(collective_id=0, has_side_effects=True, vmem_limit_bytes=VMEM_LIMIT),
    )(h1, a1, a0, dy, *weights, *moments)


def unpack_gu_kernel(z, w_ref, g_ref, mg_ref, mu_ref, vg_ref, vu_ref, wg_out, wu_out, mg_out, mu_out, vg_out, vu_out):
    side, rows, cols = z.side, z.rows, z.cols
    for f in range(FLOWS):
        out = (wg_out, wu_out)[f // 2]
        col = pl.ds((f % 2) * cols, cols)
        for n in range(z.group):
            x, y = n // side, n % side
            out[0, pl.ds(n * rows, rows), col] = w_ref[0, f, n if f < 2 else y * side + x]
        m_ref, v_ref, m_out, v_out = ((mg_ref, vg_ref, mg_out, vg_out), (mu_ref, vu_ref, mu_out, vu_out))[f // 2]
        g = g_ref[0, f].astype(F32)
        _, m_out[0, :, col], v_out[0, :, col] = adamw(g, m_ref[0, :, col], v_ref[0, :, col], g)


def unpack_d_kernel(z, w_ref, g_ref, m_ref, v_ref, w_out, m_out, v_out):
    side, rows = z.side, z.rows
    for f in range(FLOWS):
        for n in range(z.group):
            x, y = n // side, n % side
            w_out[0, pl.ds((n * FLOWS + f) * rows, rows), :] = w_ref[0, f, n if f < 2 else y * side + x]
        g = g_ref[0, f].astype(F32)
        r = pl.ds(f * rows, rows)
        _, m_out[0, r, :], v_out[0, r, :] = adamw(g, m_ref[0, r, :], v_ref[0, r, :], g)


def unpack(z, w_all, g_all, moments):
    mg, mu, md, vg, vu, vd = moments
    fb, cols, rows = z.fb, z.cols, z.rows
    last = z.layers - 1

    def unit_gu(layer, j):
        return (last - layer) * z.per_layer + j

    def unit_d(layer, i):
        return (last - layer) * z.per_layer + z.gu_units + i

    def specs(unit):
        return [
            pl.BlockSpec((1, FLOWS, z.group, rows, cols), lambda n, j: (unit(n, j), 0, 0, 0, 0)),
            pl.BlockSpec((1, FLOWS, rows, cols), lambda n, j: (unit(n, j), 0, 0, 0)),
        ]

    def column(height, width):
        return pl.BlockSpec((1, height, width), lambda n, j: (n, 0, j))

    params = pltpu.CompilerParams(vmem_limit_bytes=VMEM_LIMIT)
    part = column(rows, fb)
    like = lambda t: jax.ShapeDtypeStruct(t.shape, t.dtype)
    gate = jax.ShapeDtypeStruct((z.layers, z.d, z.ff), BF16)
    down = jax.ShapeDtypeStruct((z.layers, z.ff, z.d), BF16)
    wg, wu, mg, mu, vg, vu = pl.pallas_call(
        functools.partial(unpack_gu_kernel, z),
        grid=(z.layers, z.gu_units),
        in_specs=[*specs(unit_gu), part, part, part, part],
        out_specs=(column(z.d, fb), column(z.d, fb), part, part, part, part),
        out_shape=(gate, gate, like(mg), like(mu), like(vg), like(vu)),
        name="unpack_gu",
        compiler_params=params,
    )(w_all, g_all, mg, mu, vg, vu)
    part = column(FLOWS * rows, cols)
    wd, md, vd = pl.pallas_call(
        functools.partial(unpack_d_kernel, z),
        grid=(z.layers, z.d_units),
        in_specs=[*specs(unit_d), part, part],
        out_specs=(column(z.ff, cols), part, part),
        out_shape=(down, like(md), like(vd)),
        name="unpack_d",
        compiler_params=params,
    )(w_all, g_all, md, vd)
    return wg, wu, wd, mg, mu, md, vg, vu, vd


def normed(h):
    wide = h.astype(F32)
    return (wide * scale_of(wide)).astype(BF16)


def solution(mesh):
    group = mesh.shape["dp"]

    def device_step(x, dy, wg, wu, wd, *moments):
        x, dy = x[0], dy[0]
        z = Sizes(x.shape[0], x.shape[1], wg.shape[2], wg.shape[0], group)
        a0 = normed(x)
        p = (jax.nn.silu(mm(a0, wg[0])) * mm(a0, wu[0])).astype(BF16)
        h1 = x + mm(p, wd[0]).astype(BF16)
        a1 = normed(h1)
        w_all, g_all, _, _ = train_kernel_call(z, h1, a1, a0, dy, (wg, wu, wd), moments)
        return unpack(z, w_all, g_all, moments)

    seq, own, part, out = P(("rep", "dp")), P(), P(None, "dp"), P("rep")
    return jax.shard_map(
        device_step,
        mesh=mesh,
        in_specs=(seq, seq, own, own, own, *([part] * 6)),
        out_specs=(out, out, out, *([P("rep", "dp")] * 6)),
        check_vma=False,
    )
```

time: 1260 us -> 724 us (0.57)
  waiting for transfers between devices: 692 us -> 0 us
  Pallas kernels: 0 us -> 639 us
  matrix products: 397 us -> 75.1 us
  other arithmetic: 91.1 us -> 7.76 us
  local copies, waits for them, and re-layouts: 51.2 us -> 0.01 us
  between operations: 15.2 us -> 0.84 us
    pallas_call x0 -> x3, Pallas kernels: none -> 639 us  [the longest x1 591 us: train_kernel_call(): pl.pallas_call(functools.partial(step_kernel, z), out_shape=out_shape, in...]
    unnamed x15 -> x0, waiting for transfers between devices: 376 us -> none
    dot_general x15 -> x3, matrix products: 397 us -> 75.1 us  [mm(): return lax.dot_general(a, b, (dims, ((), ())), preferred_element_type=F32)]
    reshape x3 -> x0, waiting for transfers between devices: 317 us -> none  [step(): t.reshape(-1, *t.shape[2:])]
    unnamed x4 -> x0, other arithmetic: 63.6 us -> none
    unnamed x43 -> x4, local copies, waits for them, and re-layouts: 50.6 us -> 0.01 us
    reshape x3 -> x0, other arithmetic: 16.7 us -> none  [step(): t.reshape(-1, *t.shape[2:])]
  transfers between devices with their start and end apart: 9 -> 0, of which waited for: 7 -> 0; matrix products, arithmetic and copies ran while one was open for 25% -> 0% of each run, Pallas kernels for 0% -> 0%
where the time goes in v1:
time: 724 us; the launch traced here: 723 us
  Pallas kernels  639 us (88%)
  matrix products  75.1 us (10%)
  other arithmetic  7.76 us (1%)
    pallas_call x1, Pallas kernels, train_kernel_call(): pl.pallas_call(functools.partial(step_kernel, z), out_shape=out_shape, in...  591 us
    dot_general x3, matrix products, mm(): return lax.dot_general(a, b, (dims, ((), ())), preferred_element_type=F32)  75.1 us
    pallas_call x1, Pallas kernels, unpack(): pl.pallas_call(functools.partial(unpack_gu_kernel, z), grid=(z.layers, z....  31.9 us
    pallas_call x1, Pallas kernels, unpack(): pl.pallas_call(functools.partial(unpack_d_kernel, z), grid=(z.layers, z.d...  16.1 us

profile of v1, /device:TPU:97, one launch (start us, length us, event | category | flops | bytes accessed | tf_op | source)
XLA Modules:
  0.0 722.6 jit_solution(3756847137170979943)
XLA Ops:
  0.6 3.1 fusion.1
  3.7 0.0 copy-start.1
  3.7 24.5 %fusion.8 = f32[2048,4096]{1,0:T(8,128)} fusion(bf16[2,1024,4096]{2,1,0:T(8,128)(2,1)} %wg_in.1, bf16[1,2048,1024]{2,1,0:T(8,128)(2,1)} %param.11, f32[2048]{0:T(1024)S(1)} %add_rsqrt_fusion.1), kind=kOutput, calls=%fused_computation.12 | convolution fusion | flops 17186160640 | bytes 46145536 | tf_op jit(solution)/shard_map/dot_general | solution.py:20
  28.2 0.0 copy-done.1
  28.2 27.5 %multiply_convert_fusion.clone.3.clone.5 = bf16[2048,4096]{1,0:T(8,128)(2,1)} fusion(f32[2048,4096]{1,0:T(8,128)} %fusion.8, bf16[2,1024,4096]{2,1,0:T(8,128)(2,1)} %wu_in.1, bf16[1,2048,1024]{2,1,0:T(8,128)(2,1)S(1)} %copy-done.1, f32[2048]{0:T(1024)S(1)} %add_rsqrt_fusion.1), kind=kOutput, calls=%fused_computation.clone.clone.clone.clone.clone.clone.clone.2 | convolution fusion | flops 17236492288 | bytes 62922752 | tf_op jit(solution)/shard_map/dot_general | solution.py:20
  55.8 23.1 %fusion.3 = (f32[2048]{0:T(1024)S(1)}, bf16[2048,1024]{1,0:T(8,128)(2,1)S(1)}) fusion(bf16[2,4096,1024]{2,1,0:T(8,128)(2,1)} %wd_in.1, bf16[1,2048,1024]{2,1,0:T(8,128)(2,1)S(1)} %copy-done.1, bf16[2048,4096]{1,0:T(8,128)(2,1)} %multiply_convert_fusion.clone.3.clone.5), kind=kOutput, calls=%fused_computation.8 | convolution fusion | flops 17190352896 | bytes 33562624 | tf_op jit(solution)/shard_map/dot_general | solution.py:20
  78.9 0.0 copy-start
  78.9 4.7 fusion.2
  83.6 0.0 copy-done
  83.6 590.8 %train_step.1 = (bf16[24,4,16,64,256]{4,3,2,1,0:T(8,128)(2,1)}, bf16[24,4,64,256]{3,2,1,0:T(8,128)(2,1)}, bf16[8,2048,1024]{2,1,0:T(8,128)(2,1)}, bf16[8,512,2048]{2,1,0:T(8,128)(2,1)}) custom-call(bf16[2048,1024]{1,0:T(8,128)(2,1)} %copy-done, bf16[2048,1024]{1,0:T(8,128)(2,1)} %get-tuple-element.34.a1_in, bf16[2048,1024]{1,0:T(8,128)(2,1)} %get-tuple-element.33.a0_in, ...), custom_call_target="tpu_custom_call" | custom-call | tf_op jit(solution)/shard_map/train_step/pallas_call | solution.py:506
  674.4 16.1 %unpack_d.1 = (bf16[2,4096,1024]{2,1,0:T(8,128)(2,1)}, f32[2,256,1024]{2,1,0:T(8,128)}, f32[2,256,1024]{2,1,0:T(8,128)}) custom-call(bf16[24,4,16,64,256]{4,3,2,1,0:T(8,128)(2,1)} %get-tuple-element.20.w_ref, bf16[24,4,64,256]{3,2,1,0:T(8,128)(2,1)} %get-tuple-element.21.g_ref, f32[2,256,1024]{2,1,0:T(8,128)} %m_ref.1, f32[2,256,1024]{2,1,0:T(8,128)} %v_ref.1), custom_call_target="tpu_custom_call" | custom-call | tf_op jit(solution)/shard_map/unpack_d/pallas_call | solution.py:576
  690.6 31.9 %unpack_gu.1 = (bf16[2,1024,4096]{2,1,0:T(8,128)(2,1)}, bf16[2,1024,4096]{2,1,0:T(8,128)(2,1)}, f32[2,64,4096]{2,1,0:T(8,128)}, f32[2,64,4096]{2,1,0:T(8,128)}, ...) custom-call(bf16[24,4,16,64,256]{4,3,2,1,0:T(8,128)(2,1)} %get-tuple-element.20.w_ref, ...), custom_call_target="tpu_custom_call" | custom-call | tf_op jit(solution)/shard_map/unpack_gu/pallas_call | solution.py:566
  (2 shorter events, 0.0 us)
Async XLA Ops:
  3.7 24.5 %copy-start.1 = (bf16[1,2048,1024]{2,1,0:T(8,128)(2,1)S(1)}, bf16[1,2048,1024]{2,1,0:T(8,128)(2,1)}, u32[]{:S(2)}) copy-start(bf16[1,2048,1024]{2,1,0:T(8,128)(2,1)} %param.11) | copy-start | bytes 12582916
  78.9 4.7 copy-start

commit v2 on v1

v2 whole, which is shorter than its diff:
```python
import functools
import math

import jax
import jax.numpy as jnp
from jax import lax
from jax.experimental import pallas as pl
from jax.experimental.pallas import tpu as pltpu
from jax.sharding import PartitionSpec as P

F32, BF16 = jnp.float32, jnp.bfloat16
MESH = pl.DeviceIdType.MESH
VMEM_LIMIT = 64 * 1024 * 1024 - 128 * 1024
FLOWS = 4
HOPS = 3
UNPACK = 4
SLOTS = 4
HALVES = 2


def mm(a, b, dims=((1,), (0,))):
    return lax.dot_general(a, b, (dims, ((), ())), preferred_element_type=F32)


def scale_of(wide):
    return lax.rsqrt(jnp.mean(wide**2, -1, keepdims=True) + 1e-6)


def adamw(w, m, v, g):
    m = 0.9 * m + 0.1 * g
    v = 0.95 * v + 0.05 * g * g
    step = m * lax.rsqrt(v + 1e-8) + 0.1 * w
    return (w - 0.02 * step).astype(BF16), m, v


class Sizes:
    def __init__(self, tokens, d, ff, layers, group):
        self.tokens, self.d, self.ff, self.layers, self.group = tokens, d, ff, layers, group
        self.side = math.isqrt(group)
        self.rows = d // group
        self.quarters = ff // group // self.rows
        assert self.quarters == FLOWS and self.side == HOPS + 1
        self.cols = d // 8
        self.fb = 2 * self.cols
        self.gu_units = ff // self.fb
        self.d_units = d // self.cols
        self.per_layer = self.gu_units + self.d_units
        self.units = layers * self.per_layer
        self.gu_steps = self.gu_units // UNPACK
        self.pieces = ff // d
        assert layers == 2 and ff == 2 * tokens and tokens == 2 * d and self.fb * self.pieces == d


def step_kernel(
    z,
    x_in, dy_in, wg_in, wu_in, wd_in, mg_in, mu_in, md_in, vg_in, vu_in, vd_in,
    w_out, g_out, dgu_hbm, a0_hbm,
    a, at, d, hb, da, big, wgu, wd, dgu, grads,
    hrecv, hsend, hsum, lrecv, lsend, w_new, g_own, w_old, m_old, v_old,
    hs, hr, ls, lr, als, alr, ahs, ahr, own_sem, g_sem, adam_sem, w_sem, in_sem, dgu_sem, f_sem,
):
    side, rows, cols, fb = z.side, z.rows, z.cols, z.fb
    rep, me = lax.axis_index("rep"), lax.axis_index("dp")
    cx, cy = me // side, me % side
    first = [cx, cx, cy, cy]
    second = [cy, cy, cx, cx]
    way = [1, -1, 1, -1]

    def device(x, y):
        return (rep, ((x + side) % side) * side + (y + side) % side)

    def next_on_first(f):
        return device(cx + way[f], cy) if f < 2 else device(cx, cy + way[f])

    def next_on_second(f):
        return device(cx, cy + way[f]) if f < 2 else device(cx + way[f], cy)

    def behind(at_, f, n):
        return (at_ - way[f] * n + 2 * side) % side

    def remote(src, dst, send, recv, target):
        return pltpu.make_async_remote_copy(src, dst, send, recv, device_id=target, device_id_type=MESH)

    def h_copy(u, s, f):
        par = u % 2
        src = grads.at[u % SLOTS, f, pl.ds(side * behind(first[f], f, 1), side)] if s == 0 else hsend.at[par, s - 1, f]
        return remote(src, hrecv.at[par, s, f], hs.at[par, s, f], hr.at[par, s, f], next_on_first(f))

    def l_copy(u, s, f):
        par = u % 2
        return remote(lsend.at[par, s, f], lrecv.at[par, s, f], ls.at[par, s, f], lr.at[par, s, f], next_on_second(f))

    def al_copy(u, s, f):
        par = u % 2
        place = side * first[f] + behind(second[f], f, s)
        dst = w_out.at[u, f, place]
        src = w_new.at[par, f] if s == 0 else dst
        return remote(src, dst, als.at[par, s, f], alr.at[par, s, f], next_on_second(f))

    def ah_copy(u, s, f):
        par = u % 2
        dst = w_out.at[u, f, pl.ds(side * behind(first[f], f, s), side)]
        return remote(dst, dst, ahs.at[par, s, f], ahr.at[par, s, f], next_on_first(f))

    def own_copy(u, f):
        return pltpu.make_async_copy(w_new.at[u % 2, f], w_out.at[u, f, side * first[f] + second[f]], own_sem.at[u % 2, f])

    def g_copy(u):
        return pltpu.make_async_copy(g_own.at[u % 2], g_out.at[u], g_sem.at[u % 2])

    def place_of(u):
        return z.layers - 1 - u // z.per_layer, u % z.per_layer

    def adam_loads(u, start):
        layer, k = place_of(u) if start else (0, 0)

        def go(copies):
            for c in copies:
                c.start()

        def copies_gu():
            c0 = pl.multiple_of(k * fb, fb)
            r0 = pl.multiple_of(me * rows, rows)
            out = []
            for f in range(FLOWS):
                col = pl.ds(c0 + (f % 2) * cols, cols)
                w_, m_, v_ = ((wg_in, mg_in, vg_in), (wu_in, mu_in, vu_in))[f // 2]
                out.append(pltpu.make_async_copy(w_.at[layer, pl.ds(r0, rows), col], w_old.at[f], adam_sem.at[0, f]))
                out.append(pltpu.make_async_copy(m_.at[layer, :, col], m_old.at[f], adam_sem.at[1, f]))
                out.append(pltpu.make_async_copy(v_.at[layer, :, col], v_old.at[f], adam_sem.at[2, f]))
            return out

        def copies_d():
            col = pl.ds(pl.multiple_of((k - z.gu_units) * cols, cols), cols)
            out = []
            for f in range(FLOWS):
                r0 = pl.multiple_of((me * FLOWS + f) * rows, rows)
                out.append(pltpu.make_async_copy(wd_in.at[layer, pl.ds(r0, rows), col], w_old.at[f], adam_sem.at[0, f]))
                out.append(pltpu.make_async_copy(md_in.at[layer, pl.ds(f * rows, rows), col], m_old.at[f], adam_sem.at[1, f]))
                out.append(pltpu.make_async_copy(vd_in.at[layer, pl.ds(f * rows, rows), col], v_old.at[f], adam_sem.at[2, f]))
            return out

        if start:
            pl.when(k < z.gu_units)(lambda: go(copies_gu()))
            pl.when(k >= z.gu_units)(lambda: go(copies_d()))
        else:
            for c in copies_gu():
                c.wait()

    def both(x, y):
        return x.astype(F32) + y.astype(F32)

    def h_hop(u, s):
        par, slot = u % 2, u % SLOTS
        if s:
            for f in range(FLOWS):
                h_copy(u, s - 1, f).wait_recv()
                mine = grads[slot, f, pl.ds(side * behind(first[f], f, s + 1), side)]
                hsend[par, s - 1, f] = both(hrecv[par, s - 1, f], mine).astype(BF16)
        for f in range(FLOWS):
            h_copy(u, s, f).start()
            if s == HOPS - 1:
                h_copy(u, 0, f).wait_send()

    def h_end_l_start(u):
        par, slot = u % 2, u % SLOTS
        for f in range(FLOWS):
            h_copy(u, HOPS - 1, f).wait_recv()
            hsum[par, f] = both(hrecv[par, HOPS - 1, f], grads[slot, f, pl.ds(side * first[f], side)])
            lsend[par, 0, f] = hsum[par, f, behind(second[f], f, 1)].astype(BF16)
        for f in range(FLOWS):
            l_copy(u, 0, f).start()
        for f in range(FLOWS):
            for s in range(1, HOPS):
                h_copy(u, s, f).wait_send()

    def l_hop(u, s):
        par = u % 2
        for f in range(FLOWS):
            l_copy(u, s - 1, f).wait_recv()
            lsend[par, s, f] = both(lrecv[par, s - 1, f], hsum[par, f, behind(second[f], f, s + 1)]).astype(BF16)
        for f in range(FLOWS):
            l_copy(u, s, f).start()

    def l_end_al_start(u):
        par = u % 2
        adam_loads(u, False)
        for f in range(FLOWS):
            l_copy(u, HOPS - 1, f).wait_recv()
            g = both(lrecv[par, HOPS - 1, f], hsum[par, f, second[f]]).astype(BF16)
            g_own[par, f] = g
            w_new[par, f] = adamw(w_old[f].astype(F32), m_old[f], v_old[f], g.astype(F32))[0]
        for f in range(FLOWS):
            al_copy(u, 0, f).start()
            own_copy(u, f).start()
        g_copy(u).start()
        for f in range(FLOWS):
            for s in range(HOPS):
                l_copy(u, s, f).wait_send()

    def al_hop(u, s):
        for f in range(FLOWS):
            al_copy(u, s - 1, f).wait_recv()
            al_copy(u, s, f).start()

    def al_end_ah_start(u):
        for f in range(FLOWS):
            al_copy(u, HOPS - 1, f).wait_recv()
            own_copy(u, f).wait()
            ah_copy(u, 0, f).start()
        for f in range(FLOWS):
            for s in range(HOPS):
                al_copy(u, s, f).wait_send()
        g_copy(u).wait()

    def ah_hop(u, s):
        for f in range(FLOWS):
            ah_copy(u, s - 1, f).wait_recv()
            ah_copy(u, s, f).start()

    def ah_end(u):
        for f in range(FLOWS):
            ah_copy(u, HOPS - 1, f).wait_recv()
            for s in range(HOPS):
                ah_copy(u, s, f).wait_send()

    def if_unit(u, step):
        pl.when((u >= 0) & (u < z.units))(lambda: step(u))

    def slot_0(h):
        if_unit(h, lambda u: h_hop(u, 0))
        if_unit(h - 8, ah_end)
        if_unit(h - 6, al_end_ah_start)
        if_unit(h - 4, l_end_al_start)
        if_unit(h - 2, h_end_l_start)

    def slot_1(h):
        if_unit(h - 1, lambda u: h_hop(u, 2))
        if_unit(h - 3, lambda u: l_hop(u, 2))
        if_unit(h - 5, lambda u: al_hop(u, 2))
        if_unit(h - 7, lambda u: ah_hop(u, 2))
        if_unit(h - 3, lambda u: adam_loads(u, True))

    def slot_2(h):
        if_unit(h, lambda u: h_hop(u, 1))
        if_unit(h - 2, lambda u: l_hop(u, 1))
        if_unit(h - 4, lambda u: al_hop(u, 1))
        if_unit(h - 6, lambda u: ah_hop(u, 1))

    tile = z.tokens // HALVES
    last = z.layers - 1
    n_gu, n_d = z.gu_units, z.d_units
    a_end = n_gu - 1
    c_end = a_end + n_d
    a2_end = c_end + n_gu
    c2_end = a2_end + n_d
    wide_tile = z.tokens // 8

    def rows_of(t, size):
        return pl.ds(pl.multiple_of(t * size, size), size)

    def loop(lo, hi, body):
        lax.fori_loop(lo, hi, lambda i, c: (body(i), c)[1], 0)

    def weight_loads(layer, j, with_down):
        buf, cols_j = j % 2, rows_of(j, fb)
        out = [
            pltpu.make_async_copy(wg_in.at[layer, :, cols_j], wgu.at[buf, :, pl.ds(0, fb)], w_sem.at[buf, 0]),
            pltpu.make_async_copy(wu_in.at[layer, :, cols_j], wgu.at[buf, :, pl.ds(fb, fb)], w_sem.at[buf, 1]),
        ]
        if with_down:
            out.append(pltpu.make_async_copy(wd_in.at[layer, cols_j, :], wd.at[buf], w_sem.at[buf, 2]))
        return out

    def dgu_load(j):
        return pltpu.make_async_copy(dgu_hbm.at[j], dgu.at[j % 2], dgu_sem.at[j % 2])

    def dgu_store(j):
        return pltpu.make_async_copy(dgu.at[j % 2], dgu_hbm.at[j], dgu_sem.at[j % 2])

    def start(copies):
        for c in copies:
            c.start()

    def wait(copies):
        for c in copies:
            c.wait()

    def normed_of(wide):
        return (wide * scale_of(wide)).astype(BF16)

    def f1_block(j):
        wait(weight_loads(0, j, False))
        gu = mm(a[...], wgu[j % 2])
        gate, up = gu[:, :fb], gu[:, fb:]
        c0 = j * fb
        big[rows_of(c0 // z.tokens, z.tokens), pl.ds(pl.multiple_of(c0 % z.tokens, fb), fb)] = (jax.nn.silu(gate) * up).astype(BF16)
        pl.when(j + 2 < n_gu)(lambda: start(weight_loads(0, j + 2, False)))
        pl.when(j + 2 >= n_gu)(lambda: start(weight_loads(last, j + 2 - n_gu, True)))

    def f2_loads(n):
        buf = n % 2
        out = []
        for k in range(z.pieces):
            dst = at.at[:, pl.ds(pl.multiple_of(buf * d_half + k * fb, fb), fb)]
            out.append(pltpu.make_async_copy(wd_in.at[0, pl.ds(k * z.d, z.d), rows_of(n, fb)], dst, f_sem.at[buf, k]))
        return out

    d_half = z.tokens // 2

    def f2_block(n):
        wait(f2_loads(n))

        def part(t):
            acc = None
            for k in range(z.pieces):
                r = pl.ds(pl.multiple_of((k // 2) * z.tokens + t * tile, tile), tile)
                w_k = at[:, pl.ds(pl.multiple_of((n % 2) * d_half + k * fb, fb), fb)]
                one = mm(big[r, pl.ds((k % 2) * z.d, z.d)], w_k)
                acc = one if acc is None else acc + one
            here = (rows_of(t, tile), rows_of(n, fb))
            hb[here] = both(hb[here], acc.astype(BF16)).astype(BF16)

        loop(0, HALVES, part)
        pl.when(n + 2 < z.d // fb)(lambda: start(f2_loads(n + 2)))

    def first_norm(t):
        r = rows_of(t, wide_tile)
        a[r, :] = normed_of(hb[r, :].astype(F32))

    def norm_and_transpose(t):
        r = rows_of(t, wide_tile)
        new = normed_of(hb[r, :].astype(F32))
        a[r, :] = new
        at[:, r] = new.T

    def transpose_tile(t):
        r = rows_of(t, wide_tile)
        at[:, r] = a[r, :].T

    def backward_tile(t, j):
        buf, r = j % 2, rows_of(t, tile)
        gu = mm(a[r, :], wgu[buf])
        gate, up = gu[:, :fb], gu[:, fb:]
        dp = mm(d[r, :], wd[buf], ((1,), (1,))).astype(BF16).astype(F32)
        sig = jax.nn.sigmoid(gate)
        silu = gate * sig
        big[rows_of(j, fb), r] = (silu * up).astype(BF16).T
        dgu[buf, r, pl.ds(fb, fb)] = (dp * silu).astype(BF16)
        dgu[buf, r, pl.ds(0, fb)] = (dp * up * (sig * (1 + gate * (1 - sig)))).astype(BF16)

    def store_block(slot, f, dev, value):
        x, y = dev // side, dev % side
        grads[slot, f, x * side + y if f < 2 else y * side + x] = value

    def gu_grads(layer, j, u):
        pl.when(layer == last)(lambda: dgu_store(j).start())
        out = mm(at[...], dgu[j % 2]).astype(BF16)
        for dev in range(z.group):
            for f in range(FLOWS):
                store_block(u % SLOTS, f, dev, out[dev * rows : (dev + 1) * rows, f * cols : (f + 1) * cols])

        @pl.when(layer == last)
        def _():
            dgu_store(j).wait()

            @pl.when(j + 2 < n_gu)
            def _():
                start(weight_loads(last, j + 2, True))

            @pl.when(j + 2 >= n_gu)
            def _():
                start(weight_loads(last, j + 2 - n_gu, False))
                dgu_load(j + 2 - n_gu).start()

        pl.when((layer != last) & (j + 2 < n_gu))(lambda: start(weight_loads(0, j + 2, True)))

    def d_grads(t, pair, u):
        devices = z.group // z.pieces
        out = mm(big[rows_of(t, z.d), :], d[:, rows_of(pair, 2 * cols)]).astype(BF16)
        for n in range(devices):
            for f in range(FLOWS):
                r0 = (n * FLOWS + f) * rows
                for k in range(2):
                    store_block((u + k) % SLOTS, f, t * devices + n, out[r0 : r0 + rows, k * cols : (k + 1) * cols])

    def da_block(k):
        buf = k % 2
        wait(weight_loads(last, k, False))
        dgu_load(k).wait()

        def part(t, first):
            r = rows_of(t, tile)
            new = mm(dgu[buf, r, :], wgu[buf], ((1,), (1,)))
            da[r, :] = new if first else da[r, :] + new

        pl.when(k == 0)(lambda: loop(0, HALVES, lambda t: part(t, True)))
        pl.when(k != 0)(lambda: loop(0, HALVES, lambda t: part(t, False)))

        @pl.when(k + 2 < n_gu)
        def _():
            start(weight_loads(last, k + 2, False))
            dgu_load(k + 2).start()

        pl.when(k + 2 >= n_gu)(lambda: start(weight_loads(0, k + 2 - n_gu, True)))

    def norm_backward(t):
        r = rows_of(t, wide_tile)
        wide = hb[r, :].astype(F32)
        scale = scale_of(wide)
        by_a = da[r, :].astype(BF16).astype(F32)
        inner = jnp.mean(by_a * wide, -1, keepdims=True)
        d[r, :] = both(d[r, :], (scale * by_a - wide * (scale**3 * inner)).astype(BF16)).astype(BF16)

    def a0_load():
        return pltpu.make_async_copy(a0_hbm, a, in_sem.at[0])

    per_pair = 2 * n_gu // n_d

    def piece(h, n):
        is_gu = (h < a_end) | ((h >= c_end) & (h < a2_end))
        layer, j = jnp.where(h < a_end, last, 0), jnp.where(h < a_end, h + 1, h - c_end)
        i = jnp.where(h < c_end, h - a_end, h - a2_end)
        is_d = ((h >= a_end) & (h < c_end)) | ((h >= a2_end) & (h < c2_end))
        is_da = (h >= a_end) & (h < c_end)

        if n == 0:

            @pl.when(h == c_end)
            def _():
                a0_load().wait()
                loop(0, 8, transpose_tile)

            pl.when(h == a_end)(lambda: a0_load().start())

        @pl.when(is_gu)
        def _():
            if n == 0:
                wait(weight_loads(layer, j, True))
            if n < HALVES:
                backward_tile(n, j)
            else:
                gu_grads(layer, j, h + 1)

        @pl.when(is_d & (i % 2 == 0))
        def _():
            if n < 2:
                half = z.pieces // 2
                loop(n * half, (n + 1) * half, lambda t: d_grads(t, i // 2, h + 1))

        @pl.when(is_da & (i % 2 == 1))
        def _():
            da_block((i // 2) * per_pair + 1 + n)

        if n == 2:

            @pl.when(is_da & (i % 2 == 0))
            def _():
                da_block((i // 2) * per_pair)

            @pl.when(h == c_end - 1)
            def _():
                loop(0, 8, norm_backward)

    barrier = pltpu.get_barrier_semaphore()
    for f in range(FLOWS):
        pl.semaphore_signal(barrier, inc=1, device_id=next_on_first(f), device_id_type=MESH)
    half = pl.ds(0, z.tokens // 2), pl.ds(z.tokens // 2, z.tokens // 2)
    x_loads = [pltpu.make_async_copy(x_in.at[half[n]], hb.at[half[n]], in_sem.at[n]) for n in range(2)]
    dy_load = pltpu.make_async_copy(dy_in, d, in_sem.at[0])
    a0_store = pltpu.make_async_copy(a, a0_hbm, in_sem.at[1])
    start(x_loads + weight_loads(0, 0, False))
    for n in range(2):
        x_loads[n].wait()
        loop(4 * n, 4 * n + 4, first_norm)
    a0_store.start()
    dy_load.start()
    start(weight_loads(0, 1, False) + f2_loads(0) + f2_loads(1))
    loop(0, n_gu, f1_block)
    loop(0, z.d // fb, f2_block)
    a0_store.wait()
    loop(0, 8, norm_and_transpose)
    dy_load.wait()
    wait(weight_loads(last, 0, True))
    loop(0, HALVES, lambda t: backward_tile(t, 0))
    gu_grads(last, 0, 0)
    pl.semaphore_wait(barrier, FLOWS)

    def half_step(h):
        slot_0(h)
        piece(h, 0)
        slot_1(h)
        piece(h, 1)
        slot_2(h)
        piece(h, 2)

    loop(0, z.units + 8, half_step)


def train_kernel_call(z, x, dy, weights, moments):
    side, rows, cols, fb = z.side, z.rows, z.cols, z.fb
    dma = pltpu.SemaphoreType.DMA
    hbm = pl.BlockSpec(memory_space=pl.ANY)
    out_shape = (
        jax.ShapeDtypeStruct((z.units, FLOWS, z.group, rows, cols), BF16),
        jax.ShapeDtypeStruct((z.units, FLOWS, rows, cols), BF16),
        jax.ShapeDtypeStruct((z.gu_units, z.tokens, 2 * fb), BF16),
        jax.ShapeDtypeStruct((z.tokens, z.d), BF16),
    )
    scratch = [
        pltpu.VMEM((z.tokens, z.d), BF16),
        pltpu.VMEM((z.d, z.tokens), BF16),
        pltpu.VMEM((z.tokens, z.d), BF16),
        pltpu.VMEM((z.tokens, z.d), BF16),
        pltpu.VMEM((z.tokens, z.d), F32),
        pltpu.VMEM((z.ff, z.tokens), BF16),
        pltpu.VMEM((2, z.d, 2 * fb), BF16),
        pltpu.VMEM((2, fb, z.d), BF16),
        pltpu.VMEM((2, z.tokens, 2 * fb), BF16),
        pltpu.VMEM((SLOTS, FLOWS, z.group, rows, cols), BF16),
        pltpu.VMEM((2, HOPS, FLOWS, side, rows, cols), BF16),
        pltpu.VMEM((2, HOPS - 1, FLOWS, side, rows, cols), BF16),
        pltpu.VMEM((2, FLOWS, side, rows, cols), F32),
        pltpu.VMEM((2, HOPS, FLOWS, rows, cols), BF16),
        pltpu.VMEM((2, HOPS, FLOWS, rows, cols), BF16),
        pltpu.VMEM((2, FLOWS, rows, cols), BF16),
        pltpu.VMEM((2, FLOWS, rows, cols), BF16),
        pltpu.VMEM((FLOWS, rows, cols), BF16),
        pltpu.VMEM((FLOWS, rows, cols), F32),
        pltpu.VMEM((FLOWS, rows, cols), F32),
        *[dma((2, HOPS, FLOWS)) for _ in range(8)],
        dma((2, FLOWS)),
        dma((2,)),
        dma((3, FLOWS)),
        dma((2, 3)),
        dma((2,)),
        dma((2,)),
        dma((2, z.pieces)),
    ]
    return pl.pallas_call(
        functools.partial(step_kernel, z),
        out_shape=out_shape,
        in_specs=[hbm] * 11,
        out_specs=(hbm,) * 4,
        scratch_shapes=scratch,
        name="train_step",
        compiler_params=pltpu.CompilerParams(collective_id=0, has_side_effects=True, vmem_limit_bytes=VMEM_LIMIT),
    )(x, dy, *weights, *moments)


def unpack_kernel(z, w_ref, g_ref, *refs):
    side, rows, cols = z.side, z.rows, z.cols
    mg, mu, md, vg, vu, vd, wg_out, wu_out, wd_out, *new = refs
    mg_new, mu_new, md_new, vg_new, vu_new, vd_new = new

    def step(f, k, m, v, m_new, v_new, place):
        g = g_ref[k, f].astype(F32)
        _, m_new[place], v_new[place] = adamw(g, m[place], v[place], g)

    @pl.when(pl.program_id(1) < z.gu_steps)
    def _():
        for k in range(UNPACK):
            for f in range(FLOWS):
                col = pl.ds((2 * k + f % 2) * cols, cols)
                for dev in range(z.group):
                    place = dev if f < 2 else dev % side * side + dev // side
                    (wg_out, wu_out)[f // 2][0, pl.ds(dev * rows, rows), col] = w_ref[k, f, place]
                moments = ((mg, vg, mg_new, vg_new), (mu, vu, mu_new, vu_new))[f // 2]
                step(f, k, *moments, (0, slice(None), col))

    @pl.when(pl.program_id(1) >= z.gu_steps)
    def _():
        for k in range(UNPACK):
            col = pl.ds(k * cols, cols)
            for f in range(FLOWS):
                for dev in range(z.group):
                    place = dev if f < 2 else dev % side * side + dev // side
                    wd_out[0, pl.ds((dev * FLOWS + f) * rows, rows), col] = w_ref[k, f, place]
                step(f, k, md, vd, md_new, vd_new, (0, pl.ds(f * rows, rows), col))


def unpack(z, w_all, g_all, moments):
    cols, rows = z.cols, z.rows
    steps = z.per_layer // UNPACK

    def unit(n, j):
        return (z.layers - 1 - n) * steps + j

    def gu(height):
        return pl.BlockSpec((1, height, 2 * UNPACK * cols), lambda n, j: (n, 0, jnp.minimum(j, z.gu_steps - 1)))

    def down(height):
        return pl.BlockSpec((1, height, UNPACK * cols), lambda n, j: (n, 0, jnp.maximum(j - z.gu_steps, 0)))

    specs = [gu(rows), gu(rows), down(FLOWS * rows)] * 2
    like = [jax.ShapeDtypeStruct(t.shape, t.dtype) for t in moments]
    gate = jax.ShapeDtypeStruct((z.layers, z.d, z.ff), BF16)
    return pl.pallas_call(
        functools.partial(unpack_kernel, z),
        grid=(z.layers, steps),
        in_specs=[
            pl.BlockSpec((UNPACK, FLOWS, z.group, rows, cols), lambda n, j: (unit(n, j), 0, 0, 0, 0)),
            pl.BlockSpec((UNPACK, FLOWS, rows, cols), lambda n, j: (unit(n, j), 0, 0, 0)),
            *specs,
        ],
        out_specs=(gu(z.d), gu(z.d), down(z.ff), *specs),
        out_shape=(gate, gate, jax.ShapeDtypeStruct((z.layers, z.ff, z.d), BF16), *like),
        name="unpack",
        compiler_params=pltpu.CompilerParams(vmem_limit_bytes=VMEM_LIMIT),
    )(w_all, g_all, *moments)


def solution(mesh):
    group = mesh.shape["dp"]

    def device_step(x, dy, wg, wu, wd, *moments):
        x, dy = x[0], dy[0]
        z = Sizes(x.shape[0], x.shape[1], wg.shape[2], wg.shape[0], group)
        w_all, g_all, *_ = train_kernel_call(z, x, dy, (wg, wu, wd), moments)
        return unpack(z, w_all, g_all, moments)

    seq, own, part, out = P(("rep", "dp")), P(), P(None, "dp"), P("rep")
    return jax.shard_map(
        device_step,
        mesh=mesh,
        in_specs=(seq, seq, own, own, own, *([part] * 6)),
        out_specs=(out, out, out, *([P("rep", "dp")] * 6)),
        check_vma=False,
    )
```

time: 724 us -> 656 us (0.906)
  matrix products: 75.1 us -> 0 us
  Pallas kernels: 639 us -> 650 us
  other arithmetic: 7.76 us -> 0 us
    dot_general x3 -> x0, matrix products: 75.1 us -> none  [mm(): return lax.dot_general(a, b, (dims, ((), ())), preferred_element_type=F32)]
    pallas_call x1, Pallas kernels: 591 us -> 606 us  [train_kernel_call(): pl.pallas_call(functools.partial(step_kernel, z), out_shape=out_shape, in...]
    pallas_call x2 -> x1, Pallas kernels: 48.1 us -> 44 us  [unpack(): pl.pallas_call(functools.partial(unpack_kernel, z), grid=(z.layers, steps...]
where the time goes in v2:
time: 656 us; the launch traced here: 651 us
  Pallas kernels  650 us (99%)
    pallas_call x1, Pallas kernels, train_kernel_call(): pl.pallas_call(functools.partial(step_kernel, z), out_shape=out_shape, in...  606 us
    pallas_call x1, Pallas kernels, unpack(): pl.pallas_call(functools.partial(unpack_kernel, z), grid=(z.layers, steps...  44 us

profile of v2, /device:TPU:97, one launch (start us, length us, event | category | flops | bytes accessed | tf_op | source)
XLA Modules:
  0.0 651.1 jit_solution(17560297024630694626)
XLA Ops:
  0.6 606.3 %train_step.1 = (bf16[48,4,16,64,128]{4,3,2,1,0:T(8,128)(2,1)}, bf16[48,4,64,128]{3,2,1,0:T(8,128)(2,1)}, bf16[16,2048,512]{2,1,0:T(8,128)(2,1)}, bf16[2048,1024]{1,0:T(8,128)(2,1)}) custom-call(bf16[2048,1024]{1,0:T(8,128)(2,1)} %bitcast.2, bf16[2048,1024]{1,0:T(8,128)(2,1)} %bitcast.3, bf16[2,1024,4096]{2,1,0:T(8,128)(2,1)} %wg_in.1, ...), custom_call_target="tpu_custom_call" | custom-call | tf_op jit(solution)/shard_map/train_step/pallas_call | solution.py:540
  607.0 44.0 %unpack.1 = (bf16[2,1024,4096]{2,1,0:T(8,128)(2,1)}, bf16[2,1024,4096]{2,1,0:T(8,128)(2,1)}, bf16[2,4096,1024]{2,1,0:T(8,128)(2,1)}, f32[2,64,4096]{2,1,0:T(8,12...) custom-call(bf16[48,4,16,64,128]{4,3,2,1,0:T(8,128)(2,1)} %get-tuple, ...), custom_call_target="tpu_custom_call" | custom-call | tf_op jit(solution)/shard_map/unpack/pallas_call | solution.py:598

commit v3 on v2

v3 whole, which is shorter than its diff:
```python
import functools
import math

import jax
import jax.numpy as jnp
from jax import lax
from jax.experimental import pallas as pl
from jax.experimental.pallas import tpu as pltpu
from jax.sharding import PartitionSpec as P

F32, BF16 = jnp.float32, jnp.bfloat16
MESH = pl.DeviceIdType.MESH
VMEM_LIMIT = 64 * 1024 * 1024 - 128 * 1024
FLOWS = 4
COPIES = 3
UNPACK = 4
LAST = 2
HURRIED = 2
SETS = 4
AH_SETS = 8
SLOTS = 4
HALVES = 2


def mm(a, b, dims=((1,), (0,))):
    return lax.dot_general(a, b, (dims, ((), ())), preferred_element_type=F32)


def scale_of(wide):
    return lax.rsqrt(jnp.mean(wide**2, -1, keepdims=True) + 1e-6)


def adamw(w, m, v, g):
    m = 0.9 * m + 0.1 * g
    v = 0.95 * v + 0.05 * g * g
    step = m * lax.rsqrt(v + 1e-8) + 0.1 * w
    return (w - 0.02 * step).astype(BF16), m, v


class Sizes:
    def __init__(self, tokens, d, ff, layers, group):
        self.tokens, self.d, self.ff, self.layers, self.group = tokens, d, ff, layers, group
        self.side = math.isqrt(group)
        self.rows = d // group
        self.quarters = ff // group // self.rows
        assert self.quarters == FLOWS and self.side == 4
        self.cols = d // 8
        self.fb = 2 * self.cols
        self.gu_units = ff // self.fb
        self.d_units = d // self.cols
        self.per_layer = self.gu_units + self.d_units
        self.units = layers * self.per_layer
        self.gu_steps = self.gu_units // UNPACK
        self.pieces = ff // d
        assert layers == 2 and ff == 2 * tokens and tokens == 2 * d and self.fb * self.pieces == d


def step_kernel(
    z,
    x_in, dy_in, wg_in, wu_in, wd_in, mg_in, mu_in, md_in, vg_in, vu_in, vd_in,
    w_out, g_out, dgu_hbm, a0_hbm,
    a, at, d, hb, da, big, wgu, wd, dgu, grads,
    hrecv, hsend, hsum, lrecv, lsend, w_new, g_own, w_old, m_old, v_old, lx,
    hs, hr, ls, lr, als, alr, ahs, ahr, own_sem, g_sem, adam_sem, w_sem, in_sem, dgu_sem, f_sem, x_sem,
):
    side, rows, cols, fb = z.side, z.rows, z.cols, z.fb
    rep, me = lax.axis_index("rep"), lax.axis_index("dp")
    cx, cy = me // side, me % side
    first = [cx, cx, cy, cy]
    second = [cy, cy, cx, cx]
    way = [1, -1, 1, -1]

    def device(x, y):
        return (rep, ((x + side) % side) * side + (y + side) % side)

    def on_first(f, s):
        n = way[f] * (-1 if s == 1 else 1)
        return device(cx + n, cy) if f < 2 else device(cx, cy + n)

    def on_second(f, s, far=1):
        n = way[f] * (-1 if s == 1 else far)
        return device(cx, cy + n) if f < 2 else device(cx + n, cy)

    def behind(at_, f, n):
        return (at_ - way[f] * n + 2 * side) % side

    def remote(src, dst, send, recv, target):
        return pltpu.make_async_remote_copy(src, dst, send, recv, device_id=target, device_id_type=MESH)

    def h_copy(u, s, f):
        par = u % 2
        src = hsend.at[par, f] if s == 2 else grads.at[u % SLOTS, f, pl.ds(side * behind(first[f], f, 2 - s), side)]
        return remote(src, hrecv.at[par, s, f], hs.at[par], hr.at[par, (s + 1) // 2], on_first(f, s))

    def l_copy(u, s, f):
        par = u % 2
        return remote(lsend.at[par, s, f], lrecv.at[par, s, f], ls.at[par], lr.at[par, (s + 1) // 2], on_second(f, s))

    def al_copy(u, s, f):
        k = u % SETS
        dst = w_out.at[u, f, side * first[f] + behind(second[f], f, s // 2)]
        return remote(w_new.at[u % 2, f] if s < 2 else dst, dst, als.at[k], alr.at[k, (s + 1) // 2], on_second(f, s))

    def ah_copy(u, s, f):
        k = u % AH_SETS
        dst = w_out.at[u, f, pl.ds(side * behind(first[f], f, s // 2), side)]
        return remote(dst, dst, ahs.at[k], ahr.at[k, (s + 1) // 2], on_first(f, s))

    def own_copy(u, f):
        return pltpu.make_async_copy(w_new.at[u % 2, f], w_out.at[u, f, side * first[f] + second[f]], own_sem.at[u % 2])

    def wait_for(copies, big, sem):
        size = (hrecv if big else lrecv).at[0, pl.ds(0, copies)]
        pltpu.make_async_copy(size, size, sem).wait()

    def g_copy(u):
        return pltpu.make_async_copy(g_own.at[u % 2], g_out.at[u], g_sem.at[u % 2])

    def place_of(u):
        return z.layers - 1 - u // z.per_layer, u % z.per_layer

    def adam_loads(u, start):
        layer, k = place_of(u)
        par = u % 2

        def go(copies):
            for c in copies:
                c.start()

        def copies_gu():
            c0 = pl.multiple_of(k * fb, fb)
            r0 = pl.multiple_of(me * rows, rows)
            out = []
            for f in range(FLOWS):
                col = pl.ds(c0 + (f % 2) * cols, cols)
                w_, m_, v_ = ((wg_in, mg_in, vg_in), (wu_in, mu_in, vu_in))[f // 2]
                out.append(pltpu.make_async_copy(w_.at[layer, pl.ds(r0, rows), col], w_old.at[par, f], adam_sem.at[par, 0]))
                out.append(pltpu.make_async_copy(m_.at[layer, :, col], m_old.at[par, f], adam_sem.at[par, 1]))
                out.append(pltpu.make_async_copy(v_.at[layer, :, col], v_old.at[par, f], adam_sem.at[par, 2]))
            return out

        def copies_d():
            col = pl.ds(pl.multiple_of((k - z.gu_units) * cols, cols), cols)
            out = []
            for f in range(FLOWS):
                r0 = pl.multiple_of((me * FLOWS + f) * rows, rows)
                out.append(pltpu.make_async_copy(wd_in.at[layer, pl.ds(r0, rows), col], w_old.at[par, f], adam_sem.at[par, 0]))
                out.append(pltpu.make_async_copy(md_in.at[layer, pl.ds(f * rows, rows), col], m_old.at[par, f], adam_sem.at[par, 1]))
                out.append(pltpu.make_async_copy(vd_in.at[layer, pl.ds(f * rows, rows), col], v_old.at[par, f], adam_sem.at[par, 2]))
            return out

        if start:
            pl.when(k < z.gu_units)(lambda: go(copies_gu()))
            pl.when(k >= z.gu_units)(lambda: go(copies_d()))
        else:
            for n, old in enumerate((w_old, m_old, v_old)):
                pltpu.make_async_copy(old.at[par], old.at[par], adam_sem.at[par, n]).wait()

    def start(copies):
        for c in copies:
            c.start()

    def wait(copies):
        for c in copies:
            c.wait()

    def both(x, y):
        return x.astype(F32) + y.astype(F32)

    flows = range(FLOWS)

    def group(f, n):
        return pl.ds(side * behind(first[f], f, n), side)

    def h_a(u):
        for f in flows:
            start([h_copy(u, 0, f), h_copy(u, 1, f)])

    def h_b(u):
        par = u % 2
        wait_for(1, True, hr.at[par, 0])
        for f in flows:
            hsend[par, f] = both(hrecv[par, 0, f], grads[u % SLOTS, f, group(f, 3)]).astype(BF16)
        for f in flows:
            h_copy(u, 2, f).start()

    def h_end(u):
        par = u % 2
        wait_for(2, True, hr.at[par, 1])
        for f in flows:
            hsum[par, f] = both(hrecv[par, 1, f], hrecv[par, 2, f]) + grads[u % SLOTS, f, group(f, 0)].astype(F32)

    def l_a(u):
        par = u % 2
        h_end(u)
        for f in flows:
            for s in range(2):
                lsend[par, s, f] = hsum[par, f, behind(second[f], f, 2 - s)].astype(BF16)
        for f in flows:
            start([l_copy(u, 0, f), l_copy(u, 1, f)])
        wait_for(COPIES, True, hs.at[par])

    def step_weight(u, f, total):
        par, g = u % 2, total.astype(BF16)
        g_own[par, f] = g
        w_new[par, f] = adamw(w_old[par, f].astype(F32), m_old[par, f], v_old[par, f], g.astype(F32))[0]

    def l_b(u):
        par = u % 2
        wait_for(1, False, lr.at[par, 0])
        for f in flows:
            lsend[par, 2, f] = both(lrecv[par, 0, f], hsum[par, f, behind(second[f], f, 3)]).astype(BF16)
        for f in flows:
            l_copy(u, 2, f).start()

    def al_a(u):
        par = u % 2
        adam_loads(u, False)
        wait_for(2, False, lr.at[par, 1])
        for f in flows:
            step_weight(u, f, both(lrecv[par, 1, f], lrecv[par, 2, f]) + hsum[par, f, second[f]])
        for f in flows:
            start([al_copy(u, 0, f), al_copy(u, 1, f), own_copy(u, f)])
        g_copy(u).start()
        wait_for(COPIES, False, ls.at[par])

    def al_b(u):
        wait_for(1, False, alr.at[u % SETS, 0])
        for f in flows:
            al_copy(u, 2, f).start()

    def al_end(u):
        wait_for(2, False, alr.at[u % SETS, 1])
        wait_for(COPIES, False, als.at[u % SETS])
        wait_for(1, False, own_sem.at[u % 2])
        g_copy(u).wait()

    def ah_a(u):
        for f in flows:
            start([ah_copy(u, 0, f), ah_copy(u, 1, f)])

    def ah_b(u):
        wait_for(1, True, ahr.at[u % AH_SETS, 0])
        for f in flows:
            ah_copy(u, 2, f).start()

    def ah_end(u):
        wait_for(2, True, ahr.at[u % AH_SETS, 1])
        wait_for(COPIES, True, ahs.at[u % AH_SETS])

    def if_unit(u, step, lo=0, hi=z.units):
        pl.when((u >= lo) & (u < hi))(lambda: step(u))

    def l_last(u, f):
        return remote(lsend.at[u % 2, 2, f], lx.at[u % 2, f], x_sem.at[0, u % 2], x_sem.at[1, u % 2], on_second(f, 2, 2))

    def al_last(u, s, f):
        if s < 2:
            return al_copy(u, s, f)
        dst = w_out.at[u, f, side * first[f] + second[f]]
        return remote(w_new.at[u % 2, f], dst, x_sem.at[2, u % 2], x_sem.at[3, u % 2], on_second(f, 2, 2))

    def wait_for_last(u, send, recv, far):
        wait_for(1, False, recv.at[0])
        wait_for(1, False, recv.at[1])
        wait_for(1, False, x_sem.at[far + 1, u % 2])
        wait_for(2, False, send)
        wait_for(1, False, x_sem.at[far, u % 2])

    def l_a_last(u):
        h_end(u)
        par = u % 2
        for f in flows:
            for s, n in enumerate((3, 1, 2)):
                lsend[par, s, f] = hsum[par, f, behind(second[f], f, n)].astype(BF16)
        for f in flows:
            start([l_copy(u, 0, f), l_copy(u, 1, f), l_last(u, f)])
        wait_for(COPIES, True, hs.at[par])

    def al_a_last(u):
        par = u % 2
        adam_loads(u, False)
        wait_for_last(u, ls.at[par], lr.at[par], 0)
        for f in flows:
            step_weight(u, f, both(lrecv[par, 0, f], lrecv[par, 1, f]) + both(lx[par, f], hsum[par, f, second[f]]))
        for f in flows:
            start([al_last(u, s, f) for s in range(COPIES)] + [own_copy(u, f)])
        g_copy(u).start()

    def ah_a_last(u):
        wait_for_last(u, als.at[u % SETS], alr.at[u % SETS], 2)
        wait_for(1, False, own_sem.at[u % 2])
        ah_a(u)
        g_copy(u).wait()

    last_ones = z.units - LAST
    hurried = last_ones - HURRIED

    def slot_0(h):
        if_unit(h - 2, l_b, 0, last_ones)
        if_unit(h, h_a)
        if_unit(h - 4, al_end, hurried, last_ones)
        if_unit(h - 4, ah_a, hurried, last_ones)
        if_unit(h - 2, al_a_last, last_ones)
        if_unit(h - 4, ah_end, last_ones)

    def slot_1(h):
        if_unit(h - 3, al_b, 0, last_ones)
        if_unit(h - 1, l_a, 0, last_ones)
        if_unit(h - 1, l_a_last, last_ones)
        if_unit(h - 6, ah_end, 0, hurried)
        if_unit(h - 5, ah_end, hurried, last_ones)
        if_unit(h - 4, al_end, 0, hurried)
        if_unit(h - 4, ah_a, 0, hurried)
        if_unit(h - 3, ah_b, last_ones)
        if_unit(h - 1, lambda u: adam_loads(u, True))

    def slot_2(h):
        if_unit(h, h_b)
        if_unit(h - 2, al_a, 0, last_ones)
        if_unit(h - 5, ah_b, 0, hurried)
        if_unit(h - 4, ah_b, hurried, last_ones)
        if_unit(h - 2, ah_a_last, last_ones)

    tile = z.tokens // HALVES
    last = z.layers - 1
    n_gu, n_d = z.gu_units, z.d_units
    a_end = n_gu - 1
    c_end = a_end + n_d
    a2_end = c_end + n_gu
    c2_end = a2_end + n_d
    wide_tile = z.tokens // 8

    def rows_of(t, size):
        return pl.ds(pl.multiple_of(t * size, size), size)

    def loop(lo, hi, body):
        lax.fori_loop(lo, hi, lambda i, c: (body(i), c)[1], 0)

    def weight_loads(layer, j, with_down):
        buf, cols_j = j % 2, rows_of(j, fb)
        out = [
            pltpu.make_async_copy(wg_in.at[layer, :, cols_j], wgu.at[buf, :, pl.ds(0, fb)], w_sem.at[buf, 0]),
            pltpu.make_async_copy(wu_in.at[layer, :, cols_j], wgu.at[buf, :, pl.ds(fb, fb)], w_sem.at[buf, 1]),
        ]
        if with_down:
            out.append(pltpu.make_async_copy(wd_in.at[layer, cols_j, :], wd.at[buf], w_sem.at[buf, 2]))
        return out

    def dgu_load(j):
        return pltpu.make_async_copy(dgu_hbm.at[j], dgu.at[j % 2], dgu_sem.at[j % 2])

    def dgu_store(j):
        return pltpu.make_async_copy(dgu.at[j % 2], dgu_hbm.at[j], dgu_sem.at[j % 2])

    def normed_of(wide):
        return (wide * scale_of(wide)).astype(BF16)

    def f1_block(j):
        wait(weight_loads(0, j, False))
        gu = mm(a[...], wgu[j % 2])
        gate, up = gu[:, :fb], gu[:, fb:]
        c0 = j * fb
        big[rows_of(c0 // z.tokens, z.tokens), pl.ds(pl.multiple_of(c0 % z.tokens, fb), fb)] = (jax.nn.silu(gate) * up).astype(BF16)
        pl.when(j + 2 < n_gu)(lambda: start(weight_loads(0, j + 2, False)))
        pl.when(j + 2 >= n_gu)(lambda: start(weight_loads(last, j + 2 - n_gu, True)))

    def f2_loads(n):
        buf = n % 2
        out = []
        for k in range(z.pieces):
            dst = at.at[:, pl.ds(pl.multiple_of(buf * d_half + k * fb, fb), fb)]
            out.append(pltpu.make_async_copy(wd_in.at[0, pl.ds(k * z.d, z.d), rows_of(n, fb)], dst, f_sem.at[buf]))
        return out

    d_half = z.tokens // 2

    def f2_block(n):
        both_k = at.at[:, pl.ds(0, d_half)]
        pltpu.make_async_copy(both_k, both_k, f_sem.at[n % 2]).wait()

        def part(t):
            acc = None
            for k in range(z.pieces):
                r = pl.ds(pl.multiple_of((k // 2) * z.tokens + t * tile, tile), tile)
                w_k = at[:, pl.ds(pl.multiple_of((n % 2) * d_half + k * fb, fb), fb)]
                one = mm(big[r, pl.ds((k % 2) * z.d, z.d)], w_k)
                acc = one if acc is None else acc + one
            here = (rows_of(t, tile), rows_of(n, fb))
            hb[here] = both(hb[here], acc.astype(BF16)).astype(BF16)

        loop(0, HALVES, part)
        pl.when(n + 2 < z.d // fb)(lambda: start(f2_loads(n + 2)))

    def first_norm(t):
        r = rows_of(t, wide_tile)
        a[r, :] = normed_of(hb[r, :].astype(F32))

    def norm_and_transpose(t):
        r = rows_of(t, wide_tile)
        new = normed_of(hb[r, :].astype(F32))
        a[r, :] = new
        at[:, r] = new.T

    def transpose_tile(t):
        r = rows_of(t, wide_tile)
        at[:, r] = a[r, :].T

    def backward_tile(t, j):
        buf, r = j % 2, rows_of(t, tile)
        gu = mm(a[r, :], wgu[buf])
        gate, up = gu[:, :fb], gu[:, fb:]
        dp = mm(d[r, :], wd[buf], ((1,), (1,))).astype(BF16).astype(F32)
        sig = jax.nn.sigmoid(gate)
        silu = gate * sig
        big[rows_of(j, fb), r] = (silu * up).astype(BF16).T
        dgu[buf, r, pl.ds(fb, fb)] = (dp * silu).astype(BF16)
        dgu[buf, r, pl.ds(0, fb)] = (dp * up * (sig * (1 + gate * (1 - sig)))).astype(BF16)

    def store_block(slot, f, dev, value):
        x, y = dev // side, dev % side
        grads[slot, f, x * side + y if f < 2 else y * side + x] = value

    def gu_grads(layer, j, u):
        pl.when(layer == last)(lambda: dgu_store(j).start())
        out = mm(at[...], dgu[j % 2]).astype(BF16)
        for dev in range(z.group):
            for f in range(FLOWS):
                store_block(u % SLOTS, f, dev, out[dev * rows : (dev + 1) * rows, f * cols : (f + 1) * cols])

        @pl.when(layer == last)
        def _():
            dgu_store(j).wait()

            @pl.when(j + 2 < n_gu)
            def _():
                start(weight_loads(last, j + 2, True))

            @pl.when(j + 2 >= n_gu)
            def _():
                start(weight_loads(last, j + 2 - n_gu, False))
                dgu_load(j + 2 - n_gu).start()

        pl.when((layer != last) & (j + 2 < n_gu))(lambda: start(weight_loads(0, j + 2, True)))

    def d_grads(t, pair, u):
        devices = z.group // 2
        out = mm(big[rows_of(t, z.ff // 2), :], d[:, rows_of(pair, 2 * cols)]).astype(BF16)
        for n in range(devices):
            for f in range(FLOWS):
                r0 = (n * FLOWS + f) * rows
                for k in range(2):
                    store_block((u + k) % SLOTS, f, t * devices + n, out[r0 : r0 + rows, k * cols : (k + 1) * cols])

    def da_block(k):
        buf = k % 2
        wait(weight_loads(last, k, False))
        dgu_load(k).wait()

        def part(t, first):
            r = rows_of(t, tile)
            new = mm(dgu[buf, r, :], wgu[buf], ((1,), (1,)))
            da[r, :] = new if first else da[r, :] + new

        pl.when(k == 0)(lambda: loop(0, HALVES, lambda t: part(t, True)))
        pl.when(k != 0)(lambda: loop(0, HALVES, lambda t: part(t, False)))

        @pl.when(k + 2 < n_gu)
        def _():
            start(weight_loads(last, k + 2, False))
            dgu_load(k + 2).start()

        pl.when(k + 2 >= n_gu)(lambda: start(weight_loads(0, k + 2 - n_gu, True)))

    def norm_backward(t):
        r = rows_of(t, wide_tile)
        wide = hb[r, :].astype(F32)
        scale = scale_of(wide)
        by_a = da[r, :].astype(BF16).astype(F32)
        inner = jnp.mean(by_a * wide, -1, keepdims=True)
        d[r, :] = both(d[r, :], (scale * by_a - wide * (scale**3 * inner)).astype(BF16)).astype(BF16)

    def a0_load():
        return pltpu.make_async_copy(a0_hbm, a, in_sem.at[0])

    per_pair = 2 * n_gu // n_d

    def piece(h, n):
        is_gu = (h < a_end) | ((h >= c_end) & (h < a2_end))
        layer, j = jnp.where(h < a_end, last, 0), jnp.where(h < a_end, h + 1, h - c_end)
        i = jnp.where(h < c_end, h - a_end, h - a2_end)
        is_d = ((h >= a_end) & (h < c_end)) | ((h >= a2_end) & (h < c2_end))
        is_da = (h >= a_end) & (h < c_end)

        if n == 0:

            @pl.when(h == c_end)
            def _():
                loop(4, 8, norm_backward)
                a0_load().wait()
                loop(0, 8, transpose_tile)

            pl.when(h == a_end)(lambda: a0_load().start())

        @pl.when(is_gu)
        def _():
            if n == 0:
                wait(weight_loads(layer, j, True))
            if n < HALVES:
                backward_tile(n, j)
            else:
                gu_grads(layer, j, h + 1)

        @pl.when(is_d & (i % 2 == 0))
        def _():
            if n < 2:
                d_grads(n, i // 2, h + 1)

        @pl.when(is_da & (i % 2 == 1))
        def _():
            da_block((i // 2) * per_pair + 1 + n)

        if n == 2:

            @pl.when(is_da & (i % 2 == 0))
            def _():
                da_block((i // 2) * per_pair)

            @pl.when(h == c_end - 1)
            def _():
                loop(0, 4, norm_backward)

    barrier = pltpu.get_barrier_semaphore()
    for f in range(FLOWS):
        pl.semaphore_signal(barrier, inc=1, device_id=on_first(f, 0), device_id_type=MESH)
    half = pl.ds(0, z.tokens // 2), pl.ds(z.tokens // 2, z.tokens // 2)
    x_loads = [pltpu.make_async_copy(x_in.at[half[n]], hb.at[half[n]], in_sem.at[n]) for n in range(2)]
    dy_load = pltpu.make_async_copy(dy_in, d, in_sem.at[0])
    a0_store = pltpu.make_async_copy(a, a0_hbm, in_sem.at[1])
    start(x_loads + weight_loads(0, 0, False))
    for n in range(2):
        x_loads[n].wait()
        loop(4 * n, 4 * n + 4, first_norm)
    start(weight_loads(0, 1, False))
    a0_store.start()
    start(f2_loads(0) + f2_loads(1))
    dy_load.start()
    loop(0, n_gu, f1_block)
    loop(0, z.d // fb, f2_block)
    a0_store.wait()
    loop(0, 8, norm_and_transpose)
    dy_load.wait()
    wait(weight_loads(last, 0, True))
    loop(0, HALVES, lambda t: backward_tile(t, 0))
    gu_grads(last, 0, 0)
    pl.semaphore_wait(barrier, FLOWS)

    def half_step(h):
        slot_0(h)
        piece(h, 0)
        slot_1(h)
        piece(h, 1)
        slot_2(h)
        piece(h, 2)

    loop(0, z.units + 5, half_step)


def train_kernel_call(z, x, dy, weights, moments):
    side, rows, cols, fb = z.side, z.rows, z.cols, z.fb
    dma = pltpu.SemaphoreType.DMA
    hbm = pl.BlockSpec(memory_space=pl.ANY)
    out_shape = (
        jax.ShapeDtypeStruct((z.units, FLOWS, z.group, rows, cols), BF16),
        jax.ShapeDtypeStruct((z.units, FLOWS, rows, cols), BF16),
        jax.ShapeDtypeStruct((z.gu_units, z.tokens, 2 * fb), BF16),
        jax.ShapeDtypeStruct((z.tokens, z.d), BF16),
    )
    scratch = [
        pltpu.VMEM((z.tokens, z.d), BF16),
        pltpu.VMEM((z.d, z.tokens), BF16),
        pltpu.VMEM((z.tokens, z.d), BF16),
        pltpu.VMEM((z.tokens, z.d), BF16),
        pltpu.VMEM((z.tokens, z.d), F32),
        pltpu.VMEM((z.ff, z.tokens), BF16),
        pltpu.VMEM((2, z.d, 2 * fb), BF16),
        pltpu.VMEM((2, fb, z.d), BF16),
        pltpu.VMEM((2, z.tokens, 2 * fb), BF16),
        pltpu.VMEM((SLOTS, FLOWS, z.group, rows, cols), BF16),
        pltpu.VMEM((2, COPIES, FLOWS, side, rows, cols), BF16),
        pltpu.VMEM((2, FLOWS, side, rows, cols), BF16),
        pltpu.VMEM((2, FLOWS, side, rows, cols), F32),
        pltpu.VMEM((2, COPIES, FLOWS, rows, cols), BF16),
        pltpu.VMEM((2, COPIES, FLOWS, rows, cols), BF16),
        pltpu.VMEM((2, FLOWS, rows, cols), BF16),
        pltpu.VMEM((2, FLOWS, rows, cols), BF16),
        pltpu.VMEM((2, FLOWS, rows, cols), BF16),
        pltpu.VMEM((2, FLOWS, rows, cols), F32),
        pltpu.VMEM((2, FLOWS, rows, cols), F32),
        pltpu.VMEM((2, FLOWS, rows, cols), BF16),
        *[dma((n, *two)) for n in (2, 2, SETS, AH_SETS) for two in ((), (2,))],
        dma((2,)),
        dma((2,)),
        dma((2, 3)),
        dma((2, 3)),
        dma((2,)),
        dma((2,)),
        dma((2,)),
        dma((4, 2)),
    ]
    return pl.pallas_call(
        functools.partial(step_kernel, z),
        out_shape=out_shape,
        in_specs=[hbm] * 11,
        out_specs=(hbm,) * 4,
        scratch_shapes=scratch,
        name="train_step",
        compiler_params=pltpu.CompilerParams(collective_id=0, has_side_effects=True, vmem_limit_bytes=VMEM_LIMIT),
    )(x, dy, *weights, *moments)


def unpack_kernel(z, w_all, g_all, *refs):
    side, rows, cols = z.side, z.rows, z.cols
    olds, (wg_out, wu_out, wd_out), news, rest = refs[:6], refs[6:9], refs[9:15], refs[15:]
    gu_buf, d_buf, g_buf, *moments, in_sem, out_sem, g_sem, old_sem, new_sem = rest
    gu_cols, d_cols = 2 * UNPACK * cols, UNPACK * cols
    gu_steps, d_steps = z.gu_steps, z.d_units // UNPACK
    steps = gu_steps + d_steps

    def lanes(at, n):
        return pl.ds(pl.multiple_of(at, n), n)

    def unit_of(n, c, k):
        return (z.layers - 1 - n) * z.per_layer + c * UNPACK + k

    def buffer(c):
        return gu_buf.at[c] if c < gu_steps else d_buf.at[c - gu_steps]

    def fetch(n, c):
        def unit(k):
            u = unit_of(n, c, k)
            for f in range(FLOWS):
                if c < gu_steps:
                    dst = gu_buf.at[c, f // 2, :, :, :, lanes((2 * k + f % 2) * cols, cols)]
                else:
                    dst = d_buf.at[c - gu_steps, :, :, f, :, lanes(k * cols, cols)]
                if f < 2:
                    pltpu.make_async_copy(w_all.at[u, f], dst, in_sem.at[c]).start()
                else:
                    for y in range(side):
                        pltpu.make_async_copy(w_all.at[u, f, y], dst.at[:, y], in_sem.at[c]).start()

        lax.fori_loop(0, UNPACK, lambda k, _: (unit(k), _)[1], 0)

    def stores(n, c):
        if c < gu_steps:
            place = (n, slice(None), slice(None), slice(None), pl.ds(c * gu_cols, gu_cols))
            return [
                pltpu.make_async_copy(gu_buf.at[c, k], out.at[place], out_sem.at[c, k])
                for k, out in enumerate((wg_out, wu_out))
            ]
        place = (n, slice(None), slice(None), slice(None), slice(None), pl.ds((c - gu_steps) * d_cols, d_cols))
        return [pltpu.make_async_copy(d_buf.at[c - gu_steps], wd_out.at[place], out_sem.at[c, 0])]

    def step_moments(n, c):
        def unit(k):
            u = unit_of(n, c, k)
            for f in range(FLOWS):
                g = g_buf[u, f].astype(F32)
                if c < gu_steps:
                    kind, place = f // 2, (n, slice(None), lanes(c * gu_cols + (2 * k + f % 2) * cols, cols))
                else:
                    kind, place = 2, (n, pl.ds(f * rows, rows), lanes((c - gu_steps) * d_cols + k * cols, cols))
                m, v = moments[kind], moments[kind + 3]
                _, m[place], v[place] = adamw(g, m[place], v[place], g)

        lax.fori_loop(0, UNPACK, lambda k, _: (unit(k), _)[1], 0)
        for kind in (0, 1) if c < gu_steps else (2,):
            part = pl.ds(c * gu_cols, gu_cols) if c < gu_steps else pl.ds((c - gu_steps) * d_cols, d_cols)
            for t in (kind, kind + 3):
                pltpu.make_async_copy(moments[t].at[n, :, part], news[t].at[n, :, part], new_sem.at[t]).start()

    for c in range(2):
        fetch(0, c)
    g_load = pltpu.make_async_copy(g_all, g_buf, g_sem)
    old_loads = [pltpu.make_async_copy(olds[t], moments[t], old_sem.at[t]) for t in range(6)]
    for copy in [g_load, *old_loads]:
        copy.start()
    for c in range(2, steps):
        fetch(0, c)

    def layer(n):
        for c in range(steps):
            pltpu.make_async_copy(buffer(c), buffer(c), in_sem.at[c]).wait()
            for copy in stores(n, c):
                copy.start()
            if c == 0:

                @pl.when(n == 0)
                def _():
                    for copy in [g_load, *old_loads]:
                        copy.wait()

            step_moments(n, c)
            for done in ([c - 1] if c else []) + ([c] if c == steps - 1 else []):
                for copy in stores(n, done):
                    copy.wait()
                pl.when(n + 1 < z.layers)(lambda done=done: fetch(n + 1, done))

    lax.fori_loop(0, z.layers, lambda n, _: (layer(n), _)[1], 0)
    for t in range(6):
        pltpu.make_async_copy(moments[t], news[t], new_sem.at[t]).wait()


def unpack(z, w_all, g_all, moments):
    side, rows, cols = z.side, z.rows, z.cols
    dma = pltpu.SemaphoreType.DMA
    hbm = pl.BlockSpec(memory_space=pl.ANY)
    steps = z.per_layer // UNPACK
    grid = (side, side)
    like = [jax.ShapeDtypeStruct(t.shape, t.dtype) for t in moments]
    gate = jax.ShapeDtypeStruct((z.layers, *grid, rows, z.ff), BF16)
    down = jax.ShapeDtypeStruct((z.layers, *grid, FLOWS, rows, z.d), BF16)
    wg, wu, wd, *new = pl.pallas_call(
        functools.partial(unpack_kernel, z),
        in_specs=[hbm] * 8,
        out_specs=(hbm,) * 9,
        out_shape=(gate, gate, down, *like),
        scratch_shapes=[
            pltpu.VMEM((z.gu_steps, 2, *grid, rows, 2 * UNPACK * cols), BF16),
            pltpu.VMEM((z.d_units // UNPACK, *grid, FLOWS, rows, UNPACK * cols), BF16),
            pltpu.VMEM(g_all.shape, BF16),
            *[pltpu.VMEM(t.shape, F32) for t in moments],
            dma((steps,)),
            dma((steps, 2)),
            dma,
            dma((6,)),
            dma((6,)),
        ],
        name="unpack",
        compiler_params=pltpu.CompilerParams(vmem_limit_bytes=VMEM_LIMIT),
    )(w_all.reshape(z.units, FLOWS, *grid, rows, cols), g_all, *moments)
    return wg.reshape(z.layers, z.d, z.ff), wu.reshape(z.layers, z.d, z.ff), wd.reshape(z.layers, z.ff, z.d), *new


def solution(mesh):
    group = mesh.shape["dp"]

    def device_step(x, dy, wg, wu, wd, *moments):
        x, dy = x[0], dy[0]
        z = Sizes(x.shape[0], x.shape[1], wg.shape[2], wg.shape[0], group)
        w_all, g_all, *_ = train_kernel_call(z, x, dy, (wg, wu, wd), moments)
        return unpack(z, w_all, g_all, moments)

    seq, own, part, out = P(("rep", "dp")), P(), P(None, "dp"), P("rep")
    return jax.shard_map(
        device_step,
        mesh=mesh,
        in_specs=(seq, seq, own, own, own, *([part] * 6)),
        out_specs=(out, out, out, *([P("rep", "dp")] * 6)),
        check_vma=False,
    )
```

time: 656 us -> 640 us (0.976)
  Pallas kernels: 650 us -> 637 us
    pallas_call x1, Pallas kernels: 606 us -> 596 us  [train_kernel_call(): pl.pallas_call(functools.partial(step_kernel, z), out_shape=out_shape, in...]
where the time goes in v3:
time: 640 us; the launch traced here: 637 us
  Pallas kernels  637 us (100%)
    pallas_call x1, Pallas kernels, train_kernel_call(): pl.pallas_call(functools.partial(step_kernel, z), out_shape=out_shape, in...  596 us
    pallas_call x1, Pallas kernels, unpack(): pl.pallas_call(functools.partial(unpack_kernel, z), in_specs=[hbm] * 8, o...  40.9 us

profile of v3, /device:TPU:97, one launch (start us, length us, event | category | flops | bytes accessed | tf_op | source)
XLA Modules:
  0.0 637.4 jit_solution(311719335261494293)
XLA Ops:
  0.6 595.7 %train_step.1 = (bf16[48,4,16,64,128]{4,3,2,1,0:T(8,128)(2,1)}, bf16[48,4,64,128]{3,2,1,0:T(8,128)(2,1)}, bf16[16,2048,512]{2,1,0:T(8,128)(2,1)}, bf16[2048,1024]{1,0:T(8,128)(2,1)}) custom-call(bf16[2048,1024]{1,0:T(8,128)(2,1)} %bitcast.7, bf16[2048,1024]{1,0:T(8,128)(2,1)} %bitcast.8, bf16[2,1024,4096]{2,1,0:T(8,128)(2,1)} %wg_in.1, ...), custom_call_target="tpu_custom_call" | custom-call | tf_op jit(solution)/shard_map/train_step/pallas_call | solution.py:611
  596.4 40.9 %unpack.1 = (bf16[2,4,4,64,4096]{4,3,2,1,0:T(8,128)(2,1)}, bf16[2,4,4,64,4096]{4,3,2,1,0:T(8,128)(2,1)}, bf16[2,4,4,4,64,1024]{5,4,3,2,1,0:T(8,128)(2,1)}, f32[2...) custom-call(bf16[48,4,4,4,64,128]{5,4,3,2,1,0:T(8,128)(2,1)} %bitcas, ...), custom_call_target="tpu_custom_call" | custom-call | tf_op jit(solution)/shard_map/unpack/pallas_call | solution.py:724

commit v4 on v3

--- a/solution.py
+++ b/solution.py
@@ -396,18 +396,18 @@
         r = rows_of(t, wide_tile)
         a[r, :] = normed_of(hb[r, :].astype(F32))
 
-    def norm_and_transpose(t):
+    def second_norm(t):
         r = rows_of(t, wide_tile)
-        new = normed_of(hb[r, :].astype(F32))
-        a[r, :] = new
-        at[:, r] = new.T
+        a[r, :] = normed_of(hb[r, :].astype(F32))
 
     def transpose_tile(t):
         r = rows_of(t, wide_tile)
         at[:, r] = a[r, :].T
 
-    def backward_tile(t, j):
+    def backward_tile(t, j, transpose=False):
         buf, r = j % 2, rows_of(t, tile)
+        if transpose:
+            at[:, r] = a[r, :].T
         gu = mm(a[r, :], wgu[buf])
         gate, up = gu[:, :fb], gu[:, fb:]
         dp = mm(d[r, :], wd[buf], ((1,), (1,))).astype(BF16).astype(F32)
@@ -496,7 +496,6 @@
 
             @pl.when(h == c_end)
             def _():
-                loop(4, 8, norm_backward)
                 a0_load().wait()
                 loop(0, 8, transpose_tile)
 
@@ -516,19 +515,18 @@
             if n < 2:
                 d_grads(n, i // 2, h + 1)
 
-        @pl.when(is_da & (i % 2 == 1))
+        @pl.when(is_da)
         def _():
-            da_block((i // 2) * per_pair + 1 + n)
+            odd, later = i % 2, jnp.where(i > 1, 1, 0)
+            lo = jnp.where(odd == 1, (i // 2) * per_pair + 1 + n + later, (i // 2) * per_pair + later)
+            count = odd if n < 2 else 1 + jnp.where(i == 1, 1, 0)
+            loop(lo, jnp.minimum(lo + count, n_gu), da_block)
 
         if n == 2:
-
-            @pl.when(is_da & (i % 2 == 0))
-            def _():
-                da_block((i // 2) * per_pair)
 
             @pl.when(h == c_end - 1)
             def _():
-                loop(0, 4, norm_backward)
+                loop(0, 8, norm_backward)
 
     barrier = pltpu.get_barrier_semaphore()
     for f in range(FLOWS):
@@ -548,10 +546,10 @@
     loop(0, n_gu, f1_block)
     loop(0, z.d // fb, f2_block)
     a0_store.wait()
-    loop(0, 8, norm_and_transpose)
+    loop(0, 8, second_norm)
     dy_load.wait()
     wait(weight_loads(last, 0, True))
-    loop(0, HALVES, lambda t: backward_tile(t, 0))
+    loop(0, HALVES, lambda t: backward_tile(t, 0, True))
     gu_grads(last, 0, 0)
     pl.semaphore_wait(barrier, FLOWS)
 

time: 640 us -> 638 us (level)
  no operation moved by 1% of the time
where the time goes in v4:
time: 638 us; the launch traced here: 634 us
  Pallas kernels  633 us (99%)
    pallas_call x1, Pallas kernels, train_kernel_call(): pl.pallas_call(functools.partial(step_kernel, z), out_shape=out_shape, in...  592 us
    pallas_call x1, Pallas kernels, unpack(): pl.pallas_call(functools.partial(unpack_kernel, z), in_specs=[hbm] * 8, o...  40.9 us

profile of v4, /device:TPU:97, one launch (start us, length us, event | category | flops | bytes accessed | tf_op | source)
XLA Modules:
  0.0 633.9 jit_solution(882589957872951145)
XLA Ops:
  0.6 592.2 %train_step.1 = (bf16[48,4,16,64,128]{4,3,2,1,0:T(8,128)(2,1)}, bf16[48,4,64,128]{3,2,1,0:T(8,128)(2,1)}, bf16[16,2048,512]{2,1,0:T(8,128)(2,1)}, bf16[2048,1024]{1,0:T(8,128)(2,1)}) custom-call(bf16[2048,1024]{1,0:T(8,128)(2,1)} %bitcast.7, bf16[2048,1024]{1,0:T(8,128)(2,1)} %bitcast.8, bf16[2,1024,4096]{2,1,0:T(8,128)(2,1)} %wg_in.1, ...), custom_call_target="tpu_custom_call" | custom-call | tf_op jit(solution)/shard_map/train_step/pallas_call | solution.py:609
  592.9 40.9 %unpack.1 = (bf16[2,4,4,64,4096]{4,3,2,1,0:T(8,128)(2,1)}, bf16[2,4,4,64,4096]{4,3,2,1,0:T(8,128)(2,1)}, bf16[2,4,4,4,64,1024]{5,4,3,2,1,0:T(8,128)(2,1)}, f32[2...) custom-call(bf16[48,4,4,4,64,128]{5,4,3,2,1,0:T(8,128)(2,1)} %bitcas, ...), custom_call_target="tpu_custom_call" | custom-call | tf_op jit(solution)/shard_map/unpack/pallas_call | solution.py:722
